TPU v7x, 16 devices: a whole 2x2x2 slice. The times are simulated.
16 devices in a mesh: tp: 2 (over z), sp: 8 (over y, x, core).
Axes of the slice: x: 2, y: 2, z: 2, core: 2. Of those that a mesh axis runs over, the one named last changes fastest.
Arguments:
- x_tok: bfloat16 [256, 4096], replicated
- seq_lens: int32 [256], replicated
- k_cache: bfloat16 [256, 512, 8, 128], P(None, 'sp', 'tp')
- v_cache: bfloat16 [256, 512, 8, 128], P(None, 'sp', 'tp')
- g_attn: bfloat16 [4096], replicated
- w_q: bfloat16 [4096, 4096], P(None, 'tp')
- w_k: bfloat16 [4096, 1024], P(None, 'tp')
- w_v: bfloat16 [4096, 1024], P(None, 'tp')
- w_o: bfloat16 [4096, 4096], P('tp')
- g_mlp: bfloat16 [4096], replicated
- w_gate: bfloat16 [4096, 14336], P(None, 'tp')
- w_up: bfloat16 [4096, 14336], P(None, 'tp')
- w_down: bfloat16 [14336, 4096], P('tp')
Outputs:
- output 1: bfloat16 [256, 4096], replicated
- output 2: bfloat16 [256, 512, 8, 128], P(None, 'sp', 'tp')
- output 3: bfloat16 [256, 512, 8, 128], P(None, 'sp', 'tp')
All inputs are finite; a program needn't handle non-finite values.
Results may differ from a plain program's by a relative error of at most 0.0139779.
Values sent between devices are 32-bit elements.
A program may use at most 1.25 GiB of HBM per device.

v0:
```python
import jax
import jax.numpy as jnp
from jax import lax
from jax.sharding import PartitionSpec as P

ROPE_BASE = 500000.0
NORM_EPS = 1e-5


def rms_norm(x_in, norm_gain):
    x_f32 = x_in.astype(jnp.float32)
    inv_rms = lax.rsqrt(jnp.mean(x_f32 * x_f32, axis=-1, keepdims=True) + NORM_EPS)
    return (x_f32 * inv_rms * norm_gain.astype(jnp.float32)).astype(jnp.bfloat16)


def apply_rope(heads_in, positions):
    head_dim = heads_in.shape[-1]
    half_dim = head_dim // 2
    inv_freq = jnp.power(jnp.float32(ROPE_BASE), jnp.arange(half_dim, dtype=jnp.float32) * (-2.0 / head_dim))
    angles = positions.astype(jnp.float32)[:, None, None] * inv_freq
    cos_a = jnp.cos(angles)
    sin_a = jnp.sin(angles)
    heads_f32 = heads_in.astype(jnp.float32)
    first_half = heads_f32[..., :half_dim]
    second_half = heads_f32[..., half_dim:]
    rotated = jnp.concatenate([first_half * cos_a - second_half * sin_a, second_half * cos_a + first_half * sin_a], axis=-1)
    return rotated.astype(jnp.bfloat16)


def solution(mesh):
    cache_spec = P(None, "sp", "tp", None)
    col_spec = P(None, "tp")
    row_spec = P("tp", None)
    full_spec = P()

    def local_step(x_tok, seq_lens, k_blk, v_blk, g_attn, wq_loc, wk_loc, wv_loc, wo_loc, g_mlp, wg_loc, wu_loc, wd_loc):
        batch_rows, seq_blk, kv_loc, head_dim = k_blk.shape
        q_loc = wq_loc.shape[1] // head_dim
        groups = q_loc // kv_loc
        x_norm = rms_norm(x_tok, g_attn)
        q_new = jnp.dot(x_norm, wq_loc, preferred_element_type=jnp.float32).astype(jnp.bfloat16).reshape(batch_rows, q_loc, head_dim)
        k_new = jnp.dot(x_norm, wk_loc, preferred_element_type=jnp.float32).astype(jnp.bfloat16).reshape(batch_rows, kv_loc, head_dim)
        v_new = jnp.dot(x_norm, wv_loc, preferred_element_type=jnp.float32).astype(jnp.bfloat16).reshape(batch_rows, kv_loc, head_dim)
        q_rot = apply_rope(q_new, seq_lens)
        k_rot = apply_rope(k_new, seq_lens)
        local_pos = lax.axis_index("sp") * seq_blk + jnp.arange(seq_blk)
        is_new = (local_pos[None, :] == seq_lens[:, None])[:, :, None, None]
        k_out = jnp.where(is_new, k_rot[:, None], k_blk)
        v_out = jnp.where(is_new, v_new[:, None], v_blk)
        q_grp = q_rot.reshape(batch_rows, kv_loc, groups, head_dim)
        scores = jnp.einsum("bkgd,bskd->bkgs", q_grp, k_out, preferred_element_type=jnp.float32) * (head_dim ** -0.5)
        is_valid = (local_pos[None, :] <= seq_lens[:, None])[:, None, None, :]
        masked = jnp.where(is_valid, scores, -1e30)
        blk_max = jnp.max(masked, axis=-1, keepdims=True)
        weights = jnp.where(is_valid, jnp.exp(masked - blk_max), 0.0)
        blk_sum = jnp.sum(weights, axis=-1, keepdims=True)
        blk_mix = jnp.einsum("bkgs,bskd->bkgd", weights.astype(jnp.bfloat16), v_out, preferred_element_type=jnp.float32)
        glob_max = lax.pmax(blk_max, "sp")
        factor = jnp.exp(blk_max - glob_max)
        packed = lax.psum(jnp.concatenate([blk_mix * factor, blk_sum * factor], axis=-1), "sp")
        attn_out = (packed[..., :head_dim] / packed[..., head_dim:]).astype(jnp.bfloat16).reshape(batch_rows, q_loc * head_dim)
        attn_proj = lax.psum(jnp.dot(attn_out, wo_loc, preferred_element_type=jnp.float32), "tp")
        hidden = (x_tok.astype(jnp.float32) + attn_proj).astype(jnp.bfloat16)
        h_norm = rms_norm(hidden, g_mlp)
        gate_proj = jnp.dot(h_norm, wg_loc, preferred_element_type=jnp.float32).astype(jnp.bfloat16)
        up_proj = jnp.dot(h_norm, wu_loc, preferred_element_type=jnp.float32).astype(jnp.bfloat16)
        act_prod = (jax.nn.silu(gate_proj.astype(jnp.float32)) * up_proj.astype(jnp.float32)).astype(jnp.bfloat16)
        mlp_out = lax.psum(jnp.dot(act_prod, wd_loc, preferred_element_type=jnp.float32), "tp")
        y_out = (hidden.astype(jnp.float32) + mlp_out).astype(jnp.bfloat16)
        return y_out, k_out, v_out

    return jax.shard_map(local_step, mesh=mesh, in_specs=(full_spec, full_spec, cache_spec, cache_spec, full_spec, col_spec, col_spec, col_spec, row_spec, full_spec, col_spec, col_spec, row_spec), out_specs=(full_spec, cache_spec, cache_spec), check_vma=False)
```

profile of v0, /device:TPU:0, one launch (start us, length us, event | category | flops | bytes accessed | tf_op | source)
XLA Modules:
  0.0 529.8 jit_solution(16393709994531512875)
XLA Ops:
  7.2 0.0 all-reduce.4.cloned.1.call-start
  7.2 0.7 convert_element_type.85
  7.9 2.1 fusion.11
  10.0 0.7 convert_element_type.80
  10.7 0.8 broadcast_compare_fusion.1
  11.5 0.0 copy-start
  11.5 4.3 convolution_convert_fusion.3
  15.8 0.1 broadcast_in_dim.70
  15.9 0.0 copy-done
  15.9 3.5 fusion.27
  19.4 0.2 reshape.169
  19.6 0.0 slice-start
  19.6 0.0 slice-start.1
  19.6 0.0 slice-start.2
  19.6 8.5 %fusion.22 = f32[32,8,16,128]{3,1,2,0:T(8,128)S(1)} fusion(bf16[4096,2048]{1,0:T(8,128)(2,1)} %param.18, bf16[256,4096]{1,0:T(8,128)(2,1)S(1)} %copy-done, f32[4096]{0:T(1024)S(1)} %convert_element_type.80, f32[256]{0:T(256)S(1)} %add_rsqrt_fusion.1), kind=kOutput, calls=%fused_computation.41 | convolution fusion | flops 4300210176 | bytes 20988928 | tf_op jit(solution)/shard_map/dot_general | solution.py:41
  28.1 0.0 slice-start.3
  28.1 0.4 copy.48
  28.5 0.5 multiply_cosine_fusion
  29.0 0.5 subtract_convert_fusion.1
  29.5 0.8 subtract_convert_fusion
  30.3 0.4 pad_maximum_fusion.1
  30.7 0.0 slice-done
  30.7 0.0 slice-done.1
  30.7 0.0 slice-done.2
  30.7 0.0 slice-done.3
  30.7 26.8 %broadcast_select_fusion = (bf16[256,64,4,128]{3,2,1,0:T(4,128)(2,1)}, bf16[256,64,4,128]{3,2,1,0:T(4,128)(2,1)}) fusion(bf16[256,64,4,128]{3,2,1,0:T(4,128)(2,1)S(1)} %bitcast.29, pred[256,64]{1,0:T(8,128)(4,1)S(1)} %get-tuple-element.14, bf16[256,4,128]{2,1,0:T(4,128)(2,1)S(1)} %broadcast_in_dim.70, bf16[256,64,4,128]{3,2,1,0:T(4,128)(2,1)} %param.15, ...), kind=kLoop, calls=%fused_computation.4 | loop fusion | flops 16777216 | bytes 67649536 | tf_op jit(solution)/shard_map/jit(_where)/select_n | solution.py:49
  57.5 13.9 %fusion.23 = (f32[256,4,4]{2,1,0:T(4,128)S(1)}, f32[256,4,4,64]{3,2,1,0:T(4,128)}) fusion(pred[256,64]{1,0:T(8,128)(4,1)S(1)} %get-tuple-element.13, bf16[256,64,4,128]{3,2,1,0:T(4,128)(2,1)} %get-tuple-element.12, bf16[256,4,4,64]{3,2,1,0:T(4,128)(2,1)S(1)} %bitcast.32, bf16[256,4,4,64]{3,2,1,0:T(4,128)(2,1)S(1)} %bitcast.31), kind=kOutput, calls=%fused_computation.42 | convolution fusion | flops 69988352 | bytes 18907136 | tf_op jit(solution)/shard_map/bkgd,bskd->bkgs/dot_general | solution.py:51
  71.4 0.2 copy.41
  71.6 26.1 %pmax.7 = f32[256,4,4,1]{0,2,3,1:T(4,128)S(1)} all-reduce(f32[256,4,4,1]{0,2,3,1:T(4,128)S(1)} %bitcast.33), channel_id=1, replica_groups=mesh['tp'=2,'sp'=8] {'sp'}, use_global_device_ids=true, to_apply=%region_2.3 | all-reduce | flops 4096 | bytes 32768 | tf_op jit(solution)/shard_map/pmax | solution.py:58
  97.8 7.2 %fusion.35 = f32[256,4,4]{2,1,0:T(4,128)S(1)} fusion(f32[256,4,4]{2,1,0:T(4,128)S(1)} %get-tuple-element.17, f32[256,4,4,64]{3,2,1,0:T(4,128)} %get-tuple-element.18, pred[256,64]{1,0:T(8,128)(4,1)S(1)} %get-tuple-element.13), kind=kLoop, calls=%fused_computation.51 | loop fusion | flops 1306624 | bytes 1097728 | tf_op jit(solution)/shard_map/reduce_sum | solution.py:56
  105.0 0.2 copy.43
  105.2 0.3 copy.42
  105.5 1.9 copy.44
  107.4 0.0 copy-start.2
  107.4 9.0 %fusion.24 = f32[256,4,4,128]{3,2,1,0:T(4,128)S(1)} fusion(bf16[256,64,4,128]{3,2,1,0:T(4,128)(2,1)} %get-tuple-element.11, f32[256,4,4]{2,1,0:T(4,128)S(1)} %copy.42, f32[256,4,4,64]{3,2,1,0:T(4,128)} %get-tuple-element.18, f32[256,4,4]{2,1,0:T(4,128)S(1)} %get-tuple-element.17, pred[256,64]{1,0:T(8,128)(4,1)S(1)} %get-tuple-element.13), kind=kOutput, calls=%fused_computation.43 | convolution fusion | flops 68943872 | bytes 19972096 | tf_op jit(solution)/shard_map/bkgs,bskd->bkgd/dot_general | solution.py:57
  116.4 0.0 copy-done.2
  116.4 3.2 pad_maximum_fusion
  119.6 0.0 all-reduce.4.cloned.1.call-update
  119.6 0.0 all-reduce.6.cloned.1.call-start
  119.7 72.2 %all-reduce.4.cloned.1.call-done = f32[256,4,4,129]{3,2,1,0:T(4,128)} async-done(((f32[256,4,4,129]{3,2,1,0:T(4,128)}), f32[256,4,4,129]{3,2,1,0:T(4,128)}) %all-reduce.4.cloned.1.call-update) | async-done | bytes 2113552 | tf_op jit(solution)/shard_map/psum | solution.py:60
  191.9 3.3 slice.29
  195.2 8.1 %copy.47 = f32[256,4,4,1]{2,1,0,3:T(4,128)} copy(f32[256,4,4,1]{3,2,1,0:T(4,128)} %slice.29) | data formatting | bytes 32768 | tf_op jit(solution)/shard_map/div | solution.py:61
  203.3 3.2 fusion.21
  206.4 1.6 reshape.167
  208.1 12.6 %fusion.46 = f32[256,4096]{1,0:T(8,128)} fusion(bf16[256,2048]{1,0:T(8,128)(2,1)} %reshape.167, bf16[2048,4096]{1,0:T(8,128)(2,1)} %param.21), kind=kOutput, calls=%fused_computation.71 | convolution fusion | flops 4294967296 | bytes 22020096 | tf_op jit(solution)/shard_map/dot_general | solution.py:62
  220.6 0.0 copy-start.3
  220.6 0.0 all-reduce.6.cloned.1.call-update
  220.7 0.0 all-reduce.8.cloned.1.call-start
  220.7 0.6 copy-done.3
  221.3 103.4 %all-reduce.6.cloned.1.call-done = f32[256,4096]{1,0:T(8,128)} async-done(((f32[256,4096]{1,0:T(8,128)}), f32[256,4096]{1,0:T(8,128)}) %all-reduce.6.cloned.1.call-update) | async-done | bytes 4194320 | tf_op jit(solution)/shard_map/psum | solution.py:62
  324.8 4.3 fusion.15
  329.1 0.0 copy-start.1
  329.1 32.7 %convolution_convert_fusion.1 = bf16[256,7168]{1,0:T(8,128)(2,1)} fusion(bf16[4096,7168]{1,0:T(8,128)(2,1)} %param.23, bf16[256,4096]{1,0:T(8,128)(2,1)} %get-tuple-element.4, f32[4096]{0:T(1024)S(1)} %convert_element_type.94, f32[256]{0:T(256)S(1)} %add_rsqrt_fusion), kind=kOutput, calls=%fused_computation.12 | convolution fusion | flops 15038414848 | bytes 64504832 | tf_op jit(solution)/shard_map/dot_general | solution.py:65
  361.8 0.0 copy-done.1
  361.8 27.4 %fusion.6.clone.4 = bf16[256,7168]{1,0:T(8,128)(2,1)} fusion(bf16[4096,7168]{1,0:T(8,128)(2,1)} %param.24, bf16[256,7168]{1,0:T(8,128)(2,1)} %convolution_convert_fusion.1, bf16[256,4096]{1,0:T(8,128)(2,1)S(1)} %copy-done.1, f32[4096]{0:T(1024)S(1)} %convert_element_type.94, f32[256]{0:T(256)S(1)} %add_rsqrt_fusion), kind=kOutput, calls=%fused_computation.11.clone.clone.clone.1 | convolution fusion | flops 15053094912 | bytes 68174848 | tf_op jit(solution)/shard_map/dot_general | solution.py:66
  389.2 25.5 %fusion.10 = f32[256,4096]{1,0:T(8,128)} fusion(bf16[7168,4096]{1,0:T(8,128)(2,1)} %param.25, bf16[256,7168]{1,0:T(8,128)(2,1)} %fusion.6.clone.4), kind=kOutput, calls=%fused_computation.22 | convolution fusion | flops 15032385536 | bytes 66584576 | tf_op jit(solution)/shard_map/dot_general | solution.py:68
  414.7 0.0 all-reduce.8.cloned.1.call-update
  414.8 104.0 %all-reduce.8.cloned.1.call-done = f32[256,4096]{1,0:T(8,128)} async-done(((f32[256,4096]{1,0:T(8,128)}), f32[256,4096]{1,0:T(8,128)}) %all-reduce.8.cloned.1.call-update) | async-done | bytes 4194320 | tf_op jit(solution)/shard_map/psum | solution.py:68
  518.8 4.1 fusion.18
  (7 shorter events, 0.1 us)
Async XLA Ops:
  7.2 184.7 %all-reduce.4.cloned.1.call-start = ((), (), s32[]{:S(2)}) async-start(), calls=%async_computation | async-start | bytes 8388608 | tf_op jit(solution)/shard_map/psum | solution.py:60
  11.5 4.4 copy-start
  19.6 11.1 %slice-start = ((s8[16777216]{0:T(1024)(128)(4,1)}), s8[4194304]{0:T(1024)(128)(4,1)S(1)}, s32[]{:S(2)}) async-start(s8[16777216]{0:T(1024)(128)(4,1)} %bitcast.28), calls=%async_computation.3 | async-start | bytes 8388608
  19.6 11.1 %slice-start.1 = ((s8[16777216]{0:T(1024)(128)(4,1)}), s8[4194304]{0:T(1024)(128)(4,1)S(1)}, s32[]{:S(2)}) async-start(s8[16777216]{0:T(1024)(128)(4,1)} %bitcast.28), calls=%async_computation.4 | async-start | bytes 8388608
  19.6 11.1 %slice-start.2 = ((s8[16777216]{0:T(1024)(128)(4,1)}), s8[4194304]{0:T(1024)(128)(4,1)S(1)}, s32[]{:S(2)}) async-start(s8[16777216]{0:T(1024)(128)(4,1)} %bitcast.28), calls=%async_computation.5 | async-start | bytes 8388608
  28.1 2.6 slice-start.3
  107.4 9.0 %copy-start.2 = (f32[256,4,4,1]{3,2,1,0:T(4,128)S(1)}, f32[256,4,4,1]{3,2,1,0:T(4,128)}, u32[]{:S(2)}) copy-start(f32[256,4,4,1]{3,2,1,0:T(4,128)} %copy.44) | copy-start | bytes 49156
  119.6 205.1 %all-reduce.6.cloned.1.call-start = ((), (), s32[]{:S(2)}) async-start(), calls=%async_computation.1 | async-start | bytes 8388608 | tf_op jit(solution)/shard_map/psum | solution.py:62
  220.6 0.7 copy-start.3
  220.7 298.1 %all-reduce.8.cloned.1.call-start = ((), (), s32[]{:S(2)}) async-start(), calls=%async_computation.2 | async-start | bytes 8388608 | tf_op jit(solution)/shard_map/psum | solution.py:68
  329.1 32.7 %copy-start.1 = (bf16[256,4096]{1,0:T(8,128)(2,1)S(1)}, bf16[256,4096]{1,0:T(8,128)(2,1)}, u32[]{:S(2)}) copy-start(bf16[256,4096]{1,0:T(8,128)(2,1)} %get-tuple-element.4) | copy-start | bytes 6291460
Sparse Core Ops, SparseCore 0:
  119.8 72.1 all-reduce.3
  220.8 103.9 all-reduce.5
  414.9 103.8 all-reduce.7
where the time goes:
time: 533 us; the launch traced here: 530 us
  waiting for transfers between devices  280 us (53%)
  matrix products  137 us (26%)
  other arithmetic  55.1 us (10%)
  blocking collectives  26.1 us (5%)
  local copies, waits for them, and re-layouts  16.8 us (3%)
  between operations  14.4 us (3%)
    psum x1, waiting for transfers between devices, local_step(): lax.psum(jnp.dot(act_prod, wd_loc, preferred_element_type=jnp.float32), '...  104 us
    psum x1, waiting for transfers between devices, local_step(): lax.psum(jnp.dot(attn_out, wo_loc, preferred_element_type=jnp.float32), '...  103 us
    psum x1, waiting for transfers between devices, local_step(): lax.psum(jnp.concatenate([blk_mix * factor, blk_sum * factor], axis=-1),...  72.2 us
    dot_general x1, matrix products, local_step(): jnp.dot(h_norm, wg_loc, preferred_element_type=jnp.float32)  32.7 us
    dot_general x1, matrix products, local_step(): jnp.dot(h_norm, wu_loc, preferred_element_type=jnp.float32)  27.4 us
    select_n x1, other arithmetic, local_step(): v_out = jnp.where(is_new, v_new[:, None], v_blk)  26.8 us
    pmax x1, blocking collectives, local_step(): glob_max = lax.pmax(blk_max, 'sp')  26.1 us
    dot_general x1, matrix products, local_step(): jnp.dot(act_prod, wd_loc, preferred_element_type=jnp.float32)  25.5 us
  transfers between devices with their start and end apart: 3, of which 3 were waited for; matrix products, arithmetic and copies ran while one was open for 0% of the time, Pallas kernels for 0%

commit v1 on v0

v1 whole, which is shorter than its diff:
```python
import functools

import jax
import jax.numpy as jnp
from jax import lax
from jax.experimental import pallas as pl
from jax.experimental.pallas import tpu as pltpu
from jax.sharding import PartitionSpec as P

ROPE_BASE = 500000.0
NORM_EPS = 1e-5
F32 = jnp.float32
BF16 = jnp.bfloat16
MESH = pl.DeviceIdType.MESH
VMEM_LIMIT = 67_000_000

ROWS_STEP = 16
TILE_F = 256
SLOTS = 5
CUTS = ((0, 1408), (1408, 1408), (2816, 1280))


def rms_norm(x_in, norm_gain):
    x_f32 = x_in.astype(F32)
    inv_rms = lax.rsqrt(jnp.mean(x_f32 * x_f32, axis=-1, keepdims=True) + NORM_EPS)
    return (x_f32 * inv_rms * norm_gain.astype(F32)).astype(BF16)


def apply_rope(heads_in, positions):
    head_dim = heads_in.shape[-1]
    half_dim = head_dim // 2
    inv_freq = jnp.power(F32(ROPE_BASE), jnp.arange(half_dim, dtype=F32) * (-2.0 / head_dim))
    angles = positions.astype(F32)[:, None, None] * inv_freq
    cos_a = jnp.cos(angles)
    sin_a = jnp.sin(angles)
    heads_f32 = heads_in.astype(F32)
    first_half = heads_f32[..., :half_dim]
    second_half = heads_f32[..., half_dim:]
    rotated = jnp.concatenate([first_half * cos_a - second_half * sin_a, second_half * cos_a + first_half * sin_a], axis=-1)
    return rotated.astype(BF16)


def attn_kernel(pos_ref, q_ref, kn_ref, vn_ref, k_ref, v_ref, ko_ref, vo_ref, o_ref, ml_ref):
    step = pl.program_id(0)
    rows = k_ref.shape[1]
    heads = q_ref.shape[1]
    kv = rows // 64
    group = heads // kv
    scale = q_ref.shape[2] ** -0.5
    part = step % (64 // ROWS_STEP)

    row16 = lax.broadcasted_iota(jnp.int32, (16, 128), 0)
    for b in range(ROWS_STEP):
        pos = pos_ref[step * ROWS_STEP + b]
        first = pos * kv
        start = pl.multiple_of(jnp.clip(first // 16, 0, rows // 16 - 1) * 16, 16)
        lo = first - start
        here = (row16 >= lo) & (row16 < lo + kv)
        ko_ref[b] = k_ref[b]
        vo_ref[b] = v_ref[b]
        ko_ref[b, pl.ds(start, 16), :] = jnp.where(here, kn_ref[b], k_ref[b, pl.ds(start, 16), :])
        vo_ref[b, pl.ds(start, 16), :] = jnp.where(here, vn_ref[b], v_ref[b, pl.ds(start, 16), :])

    @pl.when(part == 0)
    def _():
        ml_ref[...] = jnp.zeros_like(ml_ref)

    row_id = lax.broadcasted_iota(jnp.int32, (heads, rows), 0)
    col_id = lax.broadcasted_iota(jnp.int32, (heads, rows), 1)
    same_head = (col_id % kv) == (row_id // group)
    lane = lax.broadcasted_iota(jnp.int32, (heads, 128), 1)
    maxes = jnp.concatenate([ml_ref[0, 0, 0], ml_ref[0, 1, 0]], axis=0)
    sums = jnp.concatenate([ml_ref[0, 0, 1], ml_ref[0, 1, 1]], axis=0)
    for base in range(0, ROWS_STEP, 8):
        scores, stats = [], []
        for b in range(base, base + 8):
            s = lax.dot_general(q_ref[b], ko_ref[b], (((1,), (1,)), ((), ())), preferred_element_type=F32)
            scores.append(s * scale)
        for k, b in enumerate(range(base, base + 8)):
            pos = pos_ref[step * ROWS_STEP + b]
            valid = same_head & (col_id < (pos + 1) * kv)
            s = jnp.where(valid, scores[k], -1e30)
            m = jnp.max(s, axis=1, keepdims=True)
            w = jnp.where(valid, jnp.exp(s - m), 0.0)
            total = jnp.sum(w, axis=1, keepdims=True)
            at = lane == part * ROWS_STEP + b
            maxes = jnp.where(at, m, maxes)
            sums = jnp.where(at, total, sums)
            stats.append(w.astype(BF16))
        for k, b in enumerate(range(base, base + 8)):
            o = jnp.dot(stats[k], vo_ref[b], preferred_element_type=F32)
            o_ref[0, 0, b] = o[:8]
            o_ref[0, 1, b] = o[8:]
    ml_ref[0, 0, 0] = maxes[:8]
    ml_ref[0, 1, 0] = maxes[8:]
    ml_ref[0, 0, 1] = sums[:8]
    ml_ref[0, 1, 1] = sums[8:]


def attention(pos, q, kn, vn, k_blk, v_blk):
    batch, rows, dim = k_blk.shape
    heads = q.shape[1]
    steps = batch // ROWS_STEP
    per = 64 // ROWS_STEP
    small = pl.BlockSpec((ROWS_STEP, 16, dim), lambda t, *_: (t, 0, 0))
    cache = pl.BlockSpec((ROWS_STEP, rows, dim), lambda t, *_: (t, 0, 0))
    return pl.pallas_call(
        attn_kernel,
        name="attend",
        grid_spec=pltpu.PrefetchScalarGridSpec(
            num_scalar_prefetch=1,
            grid=(steps,),
            in_specs=[small, small, small, cache, cache],
            out_specs=[
                cache,
                cache,
                pl.BlockSpec((1, 2, ROWS_STEP, 8, dim), lambda t, *_: (t // per, 0, t % per, 0, 0)),
                pl.BlockSpec((1, 2, 2, 8, dim), lambda t, *_: (t // per, 0, 0, 0, 0)),
            ],
        ),
        out_shape=[
            jax.ShapeDtypeStruct(k_blk.shape, BF16),
            jax.ShapeDtypeStruct(v_blk.shape, BF16),
            jax.ShapeDtypeStruct((batch // 64, 2, 64, 8, dim), F32),
            jax.ShapeDtypeStruct((batch // 64, 2, 2, 8, dim), F32),
        ],
        cost_estimate=pl.CostEstimate(flops=4 * batch * heads * rows * dim, bytes_accessed=8 * batch * rows * dim, transcendentals=batch * heads * rows),
    )(pos, q, kn, vn, k_blk, v_blk)


def blend(pairs, out_ref):
    for b in range(64):
        total = None
        for weight, part in pairs:
            term = jnp.broadcast_to(weight[:, b : b + 1], (8, 128)) * part[b]
            total = term if total is None else total + term
        out_ref[b] = total


def tail_kernel(o_ref, ml_ref, x_ref, g_ref, wo_hbm, wg_hbm, wu_hbm, wd_hbm, y_ref,
                r1, rm1, snd, sndm, r2, rm2, attn, attn_bf, wo_v, part_o, got_o, sum_o, got_z, hid, zb,
                wg_v, wu_v, wd_v, acc, got_a, sum_a, got_b, yall,
                wo_sem, w_sem, s1, t1, s2, t2, so, to, sa, ta, sg, tg, sd, td):
    sp = lax.axis_index("sp")
    z = lax.axis_index("tp")
    c = sp % 2
    xx = (sp // 2) % 2
    yy = sp // 4
    chip = sp // 2
    depth = attn_bf.shape[1]
    width = wg_hbm.shape[1] // 2
    tiles = width // TILE_F

    wo_copy = pltpu.make_async_copy(wo_hbm.at[pl.ds(pl.multiple_of(c * depth, depth), depth), :], wo_v, wo_sem)
    wo_copy.start()

    def weight_copies(t, slot):
        at = pl.ds(pl.multiple_of(c * width + t * TILE_F, TILE_F), TILE_F)
        return (
            pltpu.make_async_copy(wg_hbm.at[:, at], wg_v.at[slot], w_sem.at[0, slot]),
            pltpu.make_async_copy(wu_hbm.at[:, at], wu_v.at[slot], w_sem.at[1, slot]),
            pltpu.make_async_copy(wd_hbm.at[at, :], wd_v.at[slot], w_sem.at[2, slot]),
        )

    for t in range(SLOTS):
        for copy in weight_copies(t, t):
            copy.start()

    def spi(fx, fy, fc):
        px = 1 - xx if fx else xx
        py = 1 - yy if fy else yy
        pc = 1 - c if fc else c
        return (py * 2 + px) * 2 + pc

    core_id = {"sp": spi(0, 0, 1)}
    x_id = {"sp": spi(1, 0, 0)}
    y_id = {"sp": spi(0, 1, 0)}
    d_id = {"sp": spi(1, 1, 0)}
    z_id = {"tp": 1 - z}

    barrier = pltpu.get_barrier_semaphore()
    for peer in (core_id, x_id, y_id, d_id, z_id):
        pl.semaphore_signal(barrier, inc=1, device_id=peer, device_id_type=MESH)
    pl.semaphore_wait(barrier, 5)

    def send(src, dst, send_sem, recv_sem, peer):
        return pltpu.make_async_remote_copy(src_ref=src, dst_ref=dst, send_sem=send_sem, recv_sem=recv_sem, device_id=peer, device_id_type=MESH)

    groups = [(1 - yy) * 2 + (1 - xx), yy * 2 + (1 - xx), (1 - yy) * 2 + xx, chip]
    peers = [d_id, x_id, y_id]
    first = []
    for k in range(4):
        a = send(o_ref.at[groups[k], 1 - c], r1.at[k], s1.at[0, k], t1.at[0, k], core_id)
        b = send(ml_ref.at[groups[k], 1 - c], rm1.at[k], s1.at[1, k], t1.at[1, k], core_id)
        a.start()
        b.start()
        first.append((a, b))
    second = []
    for k in range(4):
        for copy in first[k]:
            copy.wait_recv()
        m0, l0 = ml_ref[groups[k], c, 0], ml_ref[groups[k], c, 1]
        m1, l1 = rm1[k, 0], rm1[k, 1]
        m = jnp.maximum(m0, m1)
        f0, f1 = jnp.exp(m0 - m), jnp.exp(m1 - m)
        sndm[k, 0] = m
        sndm[k, 1] = f0 * l0 + f1 * l1
        blend([(f0, o_ref.at[groups[k], c]), (f1, r1.at[k])], snd.at[k])
        if k < 3:
            a = send(snd.at[k], r2.at[k], s2.at[0, k], t2.at[0, k], peers[k])
            b = send(sndm.at[k], rm2.at[k], s2.at[1, k], t2.at[1, k], peers[k])
            a.start()
            b.start()
            second.append((a, b))
    for k in (1, 2, 0):
        for copy in second[k]:
            copy.wait_recv()
    ms = [sndm[3, 0]] + [rm2[k, 0] for k in range(3)]
    ls = [sndm[3, 1]] + [rm2[k, 1] for k in range(3)]
    m = functools.reduce(jnp.maximum, ms)
    fs = [jnp.exp(v - m) for v in ms]
    total = fs[0] * ls[0] + fs[1] * ls[1] + fs[2] * ls[2] + fs[3] * ls[3]
    total = jnp.where(total > 0.0, total, 1.0)
    blend([(fs[0] / total, snd.at[3])] + [(fs[k + 1] / total, r2.at[k]) for k in range(3)], attn)
    for h in range(8):
        attn_bf[:, h * 128 : (h + 1) * 128] = attn[:, h, :].astype(BF16)

    wo_copy.wait()

    def wo_step(n, carry):
        at = pl.ds(pl.multiple_of(n * 512, 512), 512)
        part_o[:, at] = jnp.dot(attn_bf[...], wo_v[:, at], preferred_element_type=F32)
        return carry

    lax.fori_loop(0, part_o.shape[1] // 512, wo_step, 0)
    mine = pl.ds(pl.multiple_of(c * 32, 32), 32)
    other = pl.ds(pl.multiple_of((1 - c) * 32, 32), 32)
    copy_o = send(part_o.at[other], got_o, so.at[0], to.at[0], core_id)
    copy_o.start()
    copy_o.wait_recv()
    sum_o[...] = part_o[mine] + got_o[...]
    copy_z = send(sum_o, got_z, so.at[1], to.at[1], z_id)
    copy_z.start()
    copy_z.wait_recv()
    x_rows = x_ref[pl.ds(pl.multiple_of(chip * 64 + c * 32, 32), 32), :].astype(F32)
    hid[mine] = (x_rows + (sum_o[...] + got_z[...])).astype(BF16).astype(F32)
    copy_h = send(hid.at[mine], hid.at[mine], so.at[2], to.at[2], core_id)
    copy_h.start()
    copy_h.wait_recv()

    h = hid[...]
    r = lax.rsqrt(jnp.mean(h * h, axis=-1, keepdims=True) + NORM_EPS)
    zb[...] = (h * r * g_ref[...].astype(F32)).astype(BF16)
    acc[...] = jnp.zeros_like(acc)

    def mlp_step(t, carry):
        slot = lax.rem(t, SLOTS)
        for copy in weight_copies(t, slot):
            copy.wait()
        gate = jnp.dot(zb[...], wg_v[slot], preferred_element_type=F32).astype(BF16).astype(F32)
        up = jnp.dot(zb[...], wu_v[slot], preferred_element_type=F32).astype(BF16).astype(F32)
        act = (gate * jax.nn.sigmoid(gate) * up).astype(BF16)
        acc[...] += jnp.dot(act, wd_v[slot], preferred_element_type=F32)

        @pl.when(t + SLOTS < tiles)
        def _():
            for copy in weight_copies(t + SLOTS, slot):
                copy.start()

        return carry

    lax.fori_loop(0, tiles, mlp_step, 0)

    copy_a = send(acc.at[other], got_a, sa.at[0], ta.at[0], core_id)
    copy_a.start()
    copy_a.wait_recv()
    sum_a[...] = acc[mine] + got_a[...]
    zmine = pl.ds(pl.multiple_of(z * 16, 16), 16)
    zother = pl.ds(pl.multiple_of((1 - z) * 16, 16), 16)
    copy_b = send(sum_a.at[zother], got_b, sa.at[1], ta.at[1], z_id)
    copy_b.start()
    copy_b.wait_recv()

    def rows_of(flips, fc=0):
        px = 1 - xx if "x" in flips else xx
        py = 1 - yy if "y" in flips else yy
        pz = 1 - z if "z" in flips else z
        pc = 1 - c if fc else c
        block = ((py * 2 + px) * 2 + pc) * 2 + pz
        return pl.ds(pl.multiple_of(block * 16, 16), 16)

    hid16 = hid[pl.ds(pl.multiple_of(c * 32 + z * 16, 16), 16), :]
    yall[rows_of("")] = (hid16 + (sum_a[zmine] + got_b[...])).astype(BF16).astype(F32)

    ids = {"x": x_id, "y": y_id, "z": z_id}
    orders = ("xyz", "yzx", "zxy")

    def gather_copy(p, idx):
        d0, d1, d2 = orders[p]
        src = ["", "", d0, "", d0, d1, d0 + d1][idx]
        to_dim = [d0, d1, d1, d2, d2, d2, d2][idx]
        ref = yall.at[rows_of(src), pl.ds(*CUTS[p])]
        return send(ref, ref, sg.at[p, idx], tg.at[p, idx], ids[to_dim])

    def landed(p, idx):
        d0, d1, d2 = orders[p]
        return [d0, d1, d0 + d1, d2, d2 + d0, d2 + d1, d0 + d1 + d2][idx]

    def gather_wait(p, idx):
        ref = yall.at[rows_of(landed(p, idx)), pl.ds(*CUTS[p])]
        send(ref, ref, sg.at[p, idx], tg.at[p, idx], core_id).wait_recv()

    def core_copy(p, j):
        flips = "" if j == 0 else landed(p, j - 1)
        ref = yall.at[rows_of(flips), pl.ds(*CUTS[p])]
        return send(ref, ref, sd.at[p, j], td.at[p, j], core_id)

    for idx in (0, 1, 3):
        for p in range(3):
            gather_copy(p, idx).start()
    for p in range(3):
        core_copy(p, 0).start()
    for p in range(3):
        gather_wait(p, 0)
        gather_copy(p, 2).start()
        gather_copy(p, 4).start()
        core_copy(p, 1).start()
    for p in range(3):
        gather_wait(p, 1)
        gather_copy(p, 5).start()
        core_copy(p, 2).start()
    for p in range(3):
        gather_wait(p, 2)
        gather_copy(p, 6).start()
        core_copy(p, 3).start()
    for idx in (3, 4, 5, 6):
        for p in range(3):
            gather_wait(p, idx)
            core_copy(p, idx + 1).start()
    for p in range(3):
        for j in range(8):
            flips = "" if j == 0 else landed(p, j - 1)
            ref = yall.at[rows_of(flips, 1), pl.ds(*CUTS[p])]
            send(ref, ref, sd.at[p, j], td.at[p, j], core_id).wait_recv()
    y_ref[...] = yall[...].astype(BF16)

    for pair in first + second:
        for copy in pair:
            copy.wait_send()
    for copy in (copy_o, copy_z, copy_h, copy_a, copy_b):
        copy.wait_send()
    for p in range(3):
        for idx in range(7):
            gather_copy(p, idx).wait_send()
        for j in range(8):
            core_copy(p, j).wait_send()


def tail(o, ml, x_tok, g_mlp, wo, wg, wu, wd):
    batch, width = x_tok.shape
    depth = wo.shape[0] // 2
    vmem = pl.BlockSpec(memory_space=pltpu.VMEM)
    hbm = pl.BlockSpec(memory_space=pl.ANY)
    dma = pltpu.SemaphoreType.DMA
    heads = (64, 8, 128)
    stat = (2, 8, 128)
    return pl.pallas_call(
        tail_kernel,
        name="tail",
        out_shape=jax.ShapeDtypeStruct((batch, width), BF16),
        in_specs=[vmem, vmem, vmem, vmem, hbm, hbm, hbm, hbm],
        out_specs=vmem,
        scratch_shapes=[
            pltpu.VMEM((4, *heads), F32), pltpu.VMEM((4, *stat), F32),
            pltpu.VMEM((4, *heads), F32), pltpu.VMEM((4, *stat), F32),
            pltpu.VMEM((3, *heads), F32), pltpu.VMEM((3, *stat), F32),
            pltpu.VMEM(heads, F32), pltpu.VMEM((64, depth), BF16),
            pltpu.VMEM((depth, width), BF16), pltpu.VMEM((64, width), F32),
            pltpu.VMEM((32, width), F32), pltpu.VMEM((32, width), F32), pltpu.VMEM((32, width), F32),
            pltpu.VMEM((64, width), F32), pltpu.VMEM((64, width), BF16),
            pltpu.VMEM((SLOTS, width, TILE_F), BF16), pltpu.VMEM((SLOTS, width, TILE_F), BF16), pltpu.VMEM((SLOTS, TILE_F, width), BF16),
            pltpu.VMEM((64, width), F32), pltpu.VMEM((32, width), F32), pltpu.VMEM((32, width), F32), pltpu.VMEM((16, width), F32),
            pltpu.VMEM((batch, width), F32),
            dma, dma((3, SLOTS)), dma((2, 4)), dma((2, 4)), dma((2, 3)), dma((2, 3)),
            dma((3,)), dma((3,)), dma((2,)), dma((2,)), dma((3, 7)), dma((3, 7)), dma((3, 8)), dma((3, 8)),
        ],
        compiler_params=pltpu.CompilerParams(collective_id=0, has_side_effects=True, vmem_limit_bytes=VMEM_LIMIT),
        cost_estimate=pl.CostEstimate(flops=10**10, bytes_accessed=10**8, transcendentals=0),
    )(o, ml, x_tok, g_mlp, wo, wg, wu, wd)


def solution(mesh):
    cache_spec = P(None, "sp", "tp", None)
    col_spec = P(None, "tp")
    row_spec = P("tp", None)
    full_spec = P()

    def local_step(x_tok, seq_lens, k_blk, v_blk, g_attn, wq_loc, wk_loc, wv_loc, wo_loc, g_mlp, wg_loc, wu_loc, wd_loc):
        batch_rows, seq_blk, kv_loc, head_dim = k_blk.shape
        q_loc = wq_loc.shape[1] // head_dim
        x_norm = rms_norm(x_tok, g_attn)
        q_new = jnp.dot(x_norm, wq_loc, preferred_element_type=F32).astype(BF16).reshape(batch_rows, q_loc, head_dim)
        k_new = jnp.dot(x_norm, wk_loc, preferred_element_type=F32).astype(BF16).reshape(batch_rows, kv_loc, head_dim)
        v_new = jnp.dot(x_norm, wv_loc, preferred_element_type=F32).astype(BF16).reshape(batch_rows, kv_loc, head_dim)
        q_rot = apply_rope(q_new, seq_lens)
        k_rot = apply_rope(k_new, seq_lens)
        pos = seq_lens - lax.axis_index("sp") * seq_blk
        reps = 16 // kv_loc
        flat = (batch_rows, seq_blk * kv_loc, head_dim)
        k_out, v_out, o, ml = attention(
            pos, q_rot, jnp.tile(k_rot, (1, reps, 1)), jnp.tile(v_new, (1, reps, 1)), k_blk.reshape(flat), v_blk.reshape(flat)
        )
        y_out = tail(o, ml, x_tok, g_mlp.reshape(1, -1), wo_loc, wg_loc, wu_loc, wd_loc)
        return y_out, k_out.reshape(k_blk.shape), v_out.reshape(v_blk.shape)

    return jax.shard_map(local_step, mesh=mesh, in_specs=(full_spec, full_spec, cache_spec, cache_spec, full_spec, col_spec, col_spec, col_spec, row_spec, full_spec, col_spec, col_spec, row_spec), out_specs=(full_spec, cache_spec, cache_spec), check_vma=False)
```

time: 533 us -> 154 us (0.29)
  waiting for transfers between devices: 280 us -> 0 us
  Pallas kernels: 0 us -> 124 us
  matrix products: 137 us -> 13.6 us
  other arithmetic: 55.1 us -> 7.16 us
  blocking collectives: 26.1 us -> 0 us
  between operations: 14.4 us -> 0.76 us
  local copies, waits for them, and re-layouts: 16.8 us -> 8.04 us
    psum x3 -> x0, waiting for transfers between devices: 280 us -> none  [the longest x1 104 us: local_step(): lax.psum(jnp.dot(act_prod, wd_loc, preferred_element_type=jnp.float32), '...]
    pallas_call x0 -> x2, Pallas kernels: none -> 124 us  [the longest x1 90.2 us: tail(): pl.pallas_call(tail_kernel, name='tail', out_shape=jax.ShapeDtypeStruct((...]
    dot_general x9 -> x3, matrix products: 137 us -> 13.6 us  [the longest x1 8.78 us: local_step(): jnp.dot(x_norm, wq_loc, preferred_element_type=F32).astype(BF16)]
    select_n x1 -> x0, other arithmetic: 26.8 us -> none  [local_step(): v_out = jnp.where(is_new, v_new[:, None], v_blk)]
    pmax x1 -> x0, blocking collectives: 26.1 us -> none  [local_step(): glob_max = lax.pmax(blk_max, 'sp')]
    div x1 -> x0, local copies, waits for them, and re-layouts: 8.09 us -> none  [local_step(): packed[..., :head_dim] / packed[..., head_dim:]]
    convert_element_type x5 -> x2, other arithmetic: 8.62 us -> 1.28 us  [the longest x1 0.7 us: rms_norm(): return (x_f32 * inv_rms * norm_gain.astype(F32)).astype(BF16)]
    reduce_sum x1 -> x0, other arithmetic: 7.18 us -> none  [local_step(): blk_sum = jnp.sum(weights, axis=-1, keepdims=True)]
  transfers between devices with their start and end apart: 3 -> 0, of which waited for: 3 -> 0; matrix products, arithmetic and copies ran while one was open for 0% -> 0% of each run, Pallas kernels for 0% -> 0%
where the time goes in v1:
time: 154 us; the launch traced here: 153 us
  Pallas kernels  124 us (81%)
  matrix products  13.6 us (9%)
  local copies, waits for them, and re-layouts  8.04 us (5%)
  other arithmetic  7.16 us (5%)
    pallas_call x1, Pallas kernels, tail(): pl.pallas_call(tail_kernel, name='tail', out_shape=jax.ShapeDtypeStruct((...  90.2 us
    pallas_call x1, Pallas kernels, attention(): pl.pallas_call(attn_kernel, name='attend', grid_spec=pltpu.PrefetchScalar...  33.8 us
    dot_general x1, matrix products, local_step(): jnp.dot(x_norm, wq_loc, preferred_element_type=F32).astype(BF16)  8.78 us
    unnamed x12, local copies, waits for them, and re-layouts  4.62 us
    dot_general x1, matrix products, local_step(): jnp.dot(x_norm, wv_loc, preferred_element_type=F32).astype(BF16)  3.51 us

profile of v1, /device:TPU:0, one launch (start us, length us, event | category | flops | bytes accessed | tf_op | source)
XLA Modules:
  0.0 153.5 jit_solution(17638467643653749378)
XLA Ops:
  0.6 0.7 convert_element_type.41
  1.3 2.1 %fusion = f32[256]{0:T(256)S(1)} fusion(bf16[256,4096]{1,0:T(8,128)(2,1)} %x_ref.1), kind=kLoop, calls=%fused_computation.2 | loop fusion | flops 3145472 | bytes 2098176 | tf_op jit(solution)/shard_map/reduce_sum | solution.py:25
  3.4 8.8 %fusion.4 = f32[32,8,16,128]{3,1,2,0:T(8,128)S(1)} fusion(bf16[4096,2048]{1,0:T(8,128)(2,1)} %param.18, bf16[256,4096]{1,0:T(8,128)(2,1)} %x_ref.1, f32[4096]{0:T(1024)S(1)} %convert_element_type.41, f32[256]{0:T(256)S(1)} %add_rsqrt_fusion), kind=kOutput, calls=%fused_computation.9 | convolution fusion | flops 4300210176 | bytes 20988928 | tf_op jit(solution)/shard_map/dot_general | solution.py:402
  12.2 0.0 copy-start.3
  12.2 0.4 copy.16
  12.6 0.3 copy-done.3
  12.9 0.6 fusion.9
  13.5 0.5 multiply_cosine_fusion
  14.0 0.0 copy-start
  14.0 0.0 copy-start.4
  14.0 0.8 subtract_convert_fusion
  14.9 1.5 %pad_maximum_fusion.q_ref = bf16[256,16,128]{2,1,0:T(8,128)(2,1)} fusion(bf16[256,16,64]{2,1,0:T(8,128)(2,1)S(1)} %get-tuple-element.12, bf16[256,16,64]{2,1,0:T(8,128)(2,1)S(1)} %get-tuple-element.11), kind=kLoop, calls=%fused_computation.13 | loop fusion | flops 2097152 | bytes 2097152 | tf_op jit(solution)/shard_map/concatenate | solution.py:39
  16.4 0.0 copy-done
  16.4 0.8 copy-done.4
  17.2 1.3 fusion.5
  18.5 0.0 copy-start.1
  18.5 0.2 reshape.123
  18.7 0.5 subtract_convert_fusion.1
  19.2 0.4 pad_maximum_fusion.1
  19.6 1.3 tile.19
  20.9 0.0 copy-done.1
  20.9 3.5 %convolution_convert_fusion.1 = bf16[256,512]{1,0:T(8,128)(2,1)S(1)} fusion(bf16[4096,512]{1,0:T(8,128)(2,1)} %param.20, bf16[256,4096]{1,0:T(8,128)(2,1)S(1)} %copy-done.1, f32[4096]{0:T(1024)S(1)} %convert_element_type.41, f32[256]{0:T(256)S(1)} %add_rsqrt_fusion), kind=kOutput, calls=%fused_computation.10 | convolution fusion | flops 1078067200 | bytes 6571008 | tf_op jit(solution)/shard_map/dot_general | solution.py:404
  24.4 0.1 tile.21
  24.5 1.3 tile.22
  25.8 0.0 copy-start.2
  25.8 33.8 %attend.1 = (bf16[256,256,128]{2,1,0:T(8,128)(2,1)}, bf16[256,256,128]{2,1,0:T(8,128)(2,1)}, f32[4,2,64,8,128]{4,3,2,1,0:T(8,128)}, f32[4,2,2,8,128]{4,3,2,1,0:T(8,128)}) custom-call(s32[256]{0:T(256)} %get-tuple-element.18.pos_ref, bf16[256,16,128]{2,1,0:T(8,128)(2,1)} %pad_maximum_fusion.q_ref, bf16[256,16,128]{2,1,0:T(8,128)(2,1)} %bitcast.15, ...), custom_call_target="tpu_custom_call" | custom-call | flops 536870912 | bytes 67108864 | tf_op jit(solution)/shard_map/attend/pallas_call | solution.py:107
  59.5 0.0 copy-done.2
  59.5 0.6 reshape.119.g_ref
  60.1 90.2 %tail.1 = bf16[256,4096]{1,0:T(8,128)(2,1)} custom-call(f32[4,2,64,8,128]{4,3,2,1,0:T(8,128)} %get-tuple-element.7.o_ref, f32[4,2,2,8,128]{4,3,2,1,0:T(8,128)} %get-tuple-element.8.ml_ref, bf16[256,4096]{1,0:T(8,128)(2,1)} %x_ref.1, bf16[1,4096]{1,0:T(2,128)(2,1)} %reshape.119.g_ref, bf16[2048,4096]{1,0:T(8,128)(2,1)} %wo_hbm.1, bf16[4096,7168]{1,0:T(8,128)(2,1)} %wg_hbm.1, ...), custom_call_target="tpu_custom_call" | custom-call | flops 10000000000 | bytes 100000000 | tf_op jit(solution)/shard_map/tail/pallas_call | solution.py:367
  150.4 3.1 %copy.18 = bf16[256,4096]{1,0:T(8,128)(2,1)} copy(bf16[256,4096]{1,0:T(8,128)(2,1)} %tail.1) | data formatting | bytes 4194304
  (2 shorter events, 0.0 us)
Async XLA Ops:
  12.2 0.7 copy-start.3
  14.0 2.4 %copy-start = (bf16[256,4096]{1,0:T(8,128)(2,1)S(1)}, bf16[256,4096]{1,0:T(8,128)(2,1)}, u32[]{:S(2)}) copy-start(bf16[256,4096]{1,0:T(8,128)(2,1)} %x_ref.1) | copy-start | bytes 6291460
  14.0 3.2 %copy-start.4 = (bf16[4096,512]{1,0:T(8,128)(2,1)S(1)}, bf16[4096,512]{1,0:T(8,128)(2,1)}, u32[]{:S(2)}) copy-start(bf16[4096,512]{1,0:T(8,128)(2,1)} %param.19) | copy-start | bytes 12582916
  18.5 2.4 %copy-start.1 = (bf16[256,4096]{1,0:T(8,128)(2,1)S(1)}, bf16[256,4096]{1,0:T(8,128)(2,1)}, u32[]{:S(2)}) copy-start(bf16[256,4096]{1,0:T(8,128)(2,1)} %x_ref.1) | copy-start | bytes 6291460
  25.8 33.8 %copy-start.2 = (bf16[4096]{0:T(1024)(128)(2,1)S(1)}, bf16[4096]{0:T(1024)(128)(2,1)}, u32[]{:S(2)}) copy-start(bf16[4096]{0:T(1024)(128)(2,1)} %param.22) | copy-start | bytes 24580

commit v2 on v1

--- a/solution.py
+++ b/solution.py
@@ -16,116 +16,181 @@
 
 ROWS_STEP = 16
 TILE_F = 256
+RING = 6
 SLOTS = 5
 CUTS = ((0, 1408), (1408, 1408), (2816, 1280))
 
 
-def rms_norm(x_in, norm_gain):
-    x_f32 = x_in.astype(F32)
-    inv_rms = lax.rsqrt(jnp.mean(x_f32 * x_f32, axis=-1, keepdims=True) + NORM_EPS)
-    return (x_f32 * inv_rms * norm_gain.astype(F32)).astype(BF16)
-
-
-def apply_rope(heads_in, positions):
-    head_dim = heads_in.shape[-1]
-    half_dim = head_dim // 2
-    inv_freq = jnp.power(F32(ROPE_BASE), jnp.arange(half_dim, dtype=F32) * (-2.0 / head_dim))
-    angles = positions.astype(F32)[:, None, None] * inv_freq
-    cos_a = jnp.cos(angles)
-    sin_a = jnp.sin(angles)
-    heads_f32 = heads_in.astype(F32)
-    first_half = heads_f32[..., :half_dim]
-    second_half = heads_f32[..., half_dim:]
-    rotated = jnp.concatenate([first_half * cos_a - second_half * sin_a, second_half * cos_a + first_half * sin_a], axis=-1)
-    return rotated.astype(BF16)
-
-
-def attn_kernel(pos_ref, q_ref, kn_ref, vn_ref, k_ref, v_ref, ko_ref, vo_ref, o_ref, ml_ref):
-    step = pl.program_id(0)
-    rows = k_ref.shape[1]
-    heads = q_ref.shape[1]
+def front_kernel(pos_ref, x_ref, g_ref, cos_ref, sin_ref, wq_hbm, wk_hbm, wv_hbm, k_hbm, v_hbm,
+                 ko_hbm, vo_hbm, o_ref, ml_ref, xn, w_v, qf, kf, vf, kbuf, vbuf, w_sem, in_sem, out_sem):
+    batch = x_ref.shape[0]
+    rows, dim = k_hbm.shape[1:]
     kv = rows // 64
+    heads = wq_hbm.shape[1] // dim
     group = heads // kv
-    scale = q_ref.shape[2] ** -0.5
-    part = step % (64 // ROWS_STEP)
-
-    row16 = lax.broadcasted_iota(jnp.int32, (16, 128), 0)
-    for b in range(ROWS_STEP):
-        pos = pos_ref[step * ROWS_STEP + b]
-        first = pos * kv
-        start = pl.multiple_of(jnp.clip(first // 16, 0, rows // 16 - 1) * 16, 16)
-        lo = first - start
-        here = (row16 >= lo) & (row16 < lo + kv)
-        ko_ref[b] = k_ref[b]
-        vo_ref[b] = v_ref[b]
-        ko_ref[b, pl.ds(start, 16), :] = jnp.where(here, kn_ref[b], k_ref[b, pl.ds(start, 16), :])
-        vo_ref[b, pl.ds(start, 16), :] = jnp.where(here, vn_ref[b], v_ref[b, pl.ds(start, 16), :])
-
-    @pl.when(part == 0)
-    def _():
-        ml_ref[...] = jnp.zeros_like(ml_ref)
-
+    scale = dim**-0.5
+    steps = batch // ROWS_STEP
+    q_tiles, k_tiles = wq_hbm.shape[1] // 256, wk_hbm.shape[1] // 256
+
+    weights = [(wq_hbm, j) for j in range(q_tiles)] + [(wk_hbm, j) for j in range(k_tiles)] + [(wv_hbm, j) for j in range(k_tiles)]
+    for t, (ref, j) in enumerate(weights):
+        pltpu.make_async_copy(ref.at[:, pl.ds(j * 256, 256)], w_v.at[t], w_sem.at[t]).start()
+
+    def block_in(t, slot):
+        at = pl.ds(pl.multiple_of(t * ROWS_STEP, ROWS_STEP), ROWS_STEP)
+        return (
+            pltpu.make_async_copy(k_hbm.at[at], kbuf.at[slot], in_sem.at[0, slot]),
+            pltpu.make_async_copy(v_hbm.at[at], vbuf.at[slot], in_sem.at[1, slot]),
+        )
+
+    def block_out(t, slot):
+        at = pl.ds(pl.multiple_of(t * ROWS_STEP, ROWS_STEP), ROWS_STEP)
+        return (
+            pltpu.make_async_copy(kbuf.at[slot], ko_hbm.at[at], out_sem.at[0, slot]),
+            pltpu.make_async_copy(vbuf.at[slot], vo_hbm.at[at], out_sem.at[1, slot]),
+        )
+
+    for t in range(RING):
+        for copy in block_in(t, t):
+            copy.start()
+
+    def norm_step(j, carry):
+        at = pl.ds(pl.multiple_of(j * 32, 32), 32)
+        x = x_ref[at, :].astype(F32)
+        r = lax.rsqrt(jnp.mean(x * x, axis=-1, keepdims=True) + NORM_EPS)
+        xn[at, :] = (x * r * g_ref[...].astype(F32)).astype(BF16)
+        return carry
+
+    lax.fori_loop(0, batch // 32, norm_step, 0)
+
+    def project(t):
+        pltpu.make_async_copy(wk_hbm.at[:, pl.ds(0, 256)], w_v.at[t], w_sem.at[t]).wait()
+        return jnp.dot(xn[...], w_v[t], preferred_element_type=F32).astype(BF16).astype(F32)
+
+    def rotate(head):
+        return (head * cos_ref[...] + pltpu.roll(head, dim // 2, 1) * sin_ref[...]).astype(BF16).astype(F32)
+
+    def q_step(t, carry):
+        y = project(t)
+        for j in range(2):
+            qf[pl.ds(2 * t + j, batch, stride=heads), :] = rotate(y[:, j * dim : (j + 1) * dim])
+        return carry
+
+    def k_step(t, carry):
+        y = project(q_tiles + t)
+        for j in range(2):
+            head = rotate(y[:, j * dim : (j + 1) * dim])
+            for rep in range(16 // kv):
+                kf[pl.ds(rep * kv + 2 * t + j, batch, stride=16), :] = head
+        return carry
+
+    def v_step(t, carry):
+        y = project(q_tiles + k_tiles + t)
+        for j in range(2):
+            for rep in range(16 // kv):
+                vf[pl.ds(rep * kv + 2 * t + j, batch, stride=16), :] = y[:, j * dim : (j + 1) * dim]
+        return carry
+
+    lax.fori_loop(0, q_tiles, q_step, 0)
+    lax.fori_loop(0, k_tiles, k_step, 0)
+    lax.fori_loop(0, k_tiles, v_step, 0)
+
+    ml_ref[...] = jnp.zeros_like(ml_ref)
+    row16 = lax.broadcasted_iota(jnp.int32, (16, dim), 0)
     row_id = lax.broadcasted_iota(jnp.int32, (heads, rows), 0)
     col_id = lax.broadcasted_iota(jnp.int32, (heads, rows), 1)
     same_head = (col_id % kv) == (row_id // group)
+    col_id = jnp.where(same_head, col_id, rows * 1024)
     lane = lax.broadcasted_iota(jnp.int32, (heads, 128), 1)
-    maxes = jnp.concatenate([ml_ref[0, 0, 0], ml_ref[0, 1, 0]], axis=0)
-    sums = jnp.concatenate([ml_ref[0, 0, 1], ml_ref[0, 1, 1]], axis=0)
-    for base in range(0, ROWS_STEP, 8):
-        scores, stats = [], []
-        for b in range(base, base + 8):
-            s = lax.dot_general(q_ref[b], ko_ref[b], (((1,), (1,)), ((), ())), preferred_element_type=F32)
-            scores.append(s * scale)
-        for k, b in enumerate(range(base, base + 8)):
-            pos = pos_ref[step * ROWS_STEP + b]
-            valid = same_head & (col_id < (pos + 1) * kv)
-            s = jnp.where(valid, scores[k], -1e30)
-            m = jnp.max(s, axis=1, keepdims=True)
-            w = jnp.where(valid, jnp.exp(s - m), 0.0)
-            total = jnp.sum(w, axis=1, keepdims=True)
-            at = lane == part * ROWS_STEP + b
-            maxes = jnp.where(at, m, maxes)
-            sums = jnp.where(at, total, sums)
-            stats.append(w.astype(BF16))
-        for k, b in enumerate(range(base, base + 8)):
-            o = jnp.dot(stats[k], vo_ref[b], preferred_element_type=F32)
-            o_ref[0, 0, b] = o[:8]
-            o_ref[0, 1, b] = o[8:]
-    ml_ref[0, 0, 0] = maxes[:8]
-    ml_ref[0, 1, 0] = maxes[8:]
-    ml_ref[0, 0, 1] = sums[:8]
-    ml_ref[0, 1, 1] = sums[8:]
-
-
-def attention(pos, q, kn, vn, k_blk, v_blk):
-    batch, rows, dim = k_blk.shape
-    heads = q.shape[1]
-    steps = batch // ROWS_STEP
     per = 64 // ROWS_STEP
-    small = pl.BlockSpec((ROWS_STEP, 16, dim), lambda t, *_: (t, 0, 0))
-    cache = pl.BlockSpec((ROWS_STEP, rows, dim), lambda t, *_: (t, 0, 0))
+
+    def attend_step(t, carry):
+        slot = lax.rem(t, RING)
+        chip, part = lax.div(t, per), lax.rem(t, per)
+        for copy in block_in(t, slot):
+            copy.wait()
+        for b in range(ROWS_STEP):
+            first = pos_ref[t * ROWS_STEP + b] * kv
+            start = pl.multiple_of(jnp.clip(first // 16, 0, rows // 16 - 1) * 16, 16)
+            lo = first - start
+            here = (row16 >= lo) & (row16 < lo + kv)
+            new = pl.ds(pl.multiple_of((t * ROWS_STEP + b) * 16, 16), 16)
+            at = pl.ds(start, 16)
+            kbuf[slot, b, at, :] = jnp.where(here, kf[new, :].astype(BF16), kbuf[slot, b, at, :])
+            vbuf[slot, b, at, :] = jnp.where(here, vf[new, :].astype(BF16), vbuf[slot, b, at, :])
+        maxes = jnp.concatenate([ml_ref[chip, 0, 0], ml_ref[chip, 1, 0]], axis=0)
+        sums = jnp.concatenate([ml_ref[chip, 0, 1], ml_ref[chip, 1, 1]], axis=0)
+        for base in range(0, ROWS_STEP, 8):
+            scores, weights = [], []
+            for b in range(base, base + 8):
+                q = qf[pl.ds(pl.multiple_of((t * ROWS_STEP + b) * heads, heads), heads), :].astype(BF16)
+                s = lax.dot_general(q, kbuf[slot, b], (((1,), (1,)), ((), ())), preferred_element_type=F32)
+                scores.append(s * scale)
+            for n, b in enumerate(range(base, base + 8)):
+                valid = col_id < (pos_ref[t * ROWS_STEP + b] + 1) * kv
+                s = jnp.where(valid, scores[n], -1e30)
+                m = jnp.max(s, axis=1, keepdims=True)
+                w = jnp.where(valid, jnp.exp(s - m), 0.0)
+                here = lane == part * ROWS_STEP + b
+                maxes = jnp.where(here, m, maxes)
+                sums = jnp.where(here, jnp.sum(w, axis=1, keepdims=True), sums)
+                weights.append(w.astype(BF16))
+            for n, b in enumerate(range(base, base + 8)):
+                o = jnp.dot(weights[n], vbuf[slot, b], preferred_element_type=F32)
+                o_ref[chip, 0, part * ROWS_STEP + b] = o[:8]
+                o_ref[chip, 1, part * ROWS_STEP + b] = o[8:]
+        ml_ref[chip, 0, 0] = maxes[:8]
+        ml_ref[chip, 1, 0] = maxes[8:]
+        ml_ref[chip, 0, 1] = sums[:8]
+        ml_ref[chip, 1, 1] = sums[8:]
+        for copy in block_out(t, slot):
+            copy.start()
+
+        @pl.when((t >= 1) & (t - 1 + RING < steps))
+        def _():
+            before = lax.rem(t - 1, RING)
+            for copy in block_out(t - 1, before):
+                copy.wait()
+            for copy in block_in(t - 1 + RING, before):
+                copy.start()
+
+        return carry
+
+    lax.fori_loop(0, steps, attend_step, 0)
+    for t in range(steps - RING, steps):
+        for copy in block_out(t, t % RING):
+            copy.wait()
+
+
+def front(pos, x_tok, g_attn, cos2, sin2, wq, wk, wv, k_blk, v_blk):
+    batch, width = x_tok.shape
+    _, rows, dim = k_blk.shape
+    heads = wq.shape[1] // dim
+    tiles = (wq.shape[1] + wk.shape[1] + wv.shape[1]) // 256
+    vmem = pl.BlockSpec(memory_space=pltpu.VMEM)
+    hbm = pl.BlockSpec(memory_space=pl.ANY)
+    dma = pltpu.SemaphoreType.DMA
     return pl.pallas_call(
-        attn_kernel,
-        name="attend",
-        grid_spec=pltpu.PrefetchScalarGridSpec(
-            num_scalar_prefetch=1,
-            grid=(steps,),
-            in_specs=[small, small, small, cache, cache],
-            out_specs=[
-                cache,
-                cache,
-                pl.BlockSpec((1, 2, ROWS_STEP, 8, dim), lambda t, *_: (t // per, 0, t % per, 0, 0)),
-                pl.BlockSpec((1, 2, 2, 8, dim), lambda t, *_: (t // per, 0, 0, 0, 0)),
-            ],
-        ),
+        front_kernel,
+        name="front",
+        in_specs=[pl.BlockSpec(memory_space=pltpu.SMEM), vmem, vmem, vmem, vmem, hbm, hbm, hbm, hbm, hbm],
+        out_specs=[hbm, hbm, vmem, vmem],
         out_shape=[
             jax.ShapeDtypeStruct(k_blk.shape, BF16),
             jax.ShapeDtypeStruct(v_blk.shape, BF16),
             jax.ShapeDtypeStruct((batch // 64, 2, 64, 8, dim), F32),
             jax.ShapeDtypeStruct((batch // 64, 2, 2, 8, dim), F32),
         ],
-        cost_estimate=pl.CostEstimate(flops=4 * batch * heads * rows * dim, bytes_accessed=8 * batch * rows * dim, transcendentals=batch * heads * rows),
-    )(pos, q, kn, vn, k_blk, v_blk)
+        scratch_shapes=[
+            pltpu.VMEM((batch, width), BF16),
+            pltpu.VMEM((tiles, width, 256), BF16),
+            pltpu.VMEM((batch * heads, dim), F32), pltpu.VMEM((batch * 16, dim), F32), pltpu.VMEM((batch * 16, dim), F32),
+            pltpu.VMEM((RING, ROWS_STEP, rows, dim), BF16), pltpu.VMEM((RING, ROWS_STEP, rows, dim), BF16),
+            dma((tiles,)), dma((2, RING)), dma((2, RING)),
+        ],
+        compiler_params=pltpu.CompilerParams(vmem_limit_bytes=VMEM_LIMIT),
+        cost_estimate=pl.CostEstimate(flops=10**10, bytes_accessed=10**8, transcendentals=0),
+    )(pos, x_tok, g_attn, cos2, sin2, wq, wk, wv, k_blk, v_blk)
 
 
 def blend(pairs, out_ref):
@@ -397,18 +462,15 @@
 
     def local_step(x_tok, seq_lens, k_blk, v_blk, g_attn, wq_loc, wk_loc, wv_loc, wo_loc, g_mlp, wg_loc, wu_loc, wd_loc):
         batch_rows, seq_blk, kv_loc, head_dim = k_blk.shape
-        q_loc = wq_loc.shape[1] // head_dim
-        x_norm = rms_norm(x_tok, g_attn)
-        q_new = jnp.dot(x_norm, wq_loc, preferred_element_type=F32).astype(BF16).reshape(batch_rows, q_loc, head_dim)
-        k_new = jnp.dot(x_norm, wk_loc, preferred_element_type=F32).astype(BF16).reshape(batch_rows, kv_loc, head_dim)
-        v_new = jnp.dot(x_norm, wv_loc, preferred_element_type=F32).astype(BF16).reshape(batch_rows, kv_loc, head_dim)
-        q_rot = apply_rope(q_new, seq_lens)
-        k_rot = apply_rope(k_new, seq_lens)
+        half = head_dim // 2
+        inv_freq = jnp.power(F32(ROPE_BASE), jnp.arange(half, dtype=F32) * (-2.0 / head_dim))
+        angles = seq_lens.astype(F32)[:, None] * jnp.concatenate([inv_freq, inv_freq])
+        cos2 = jnp.cos(angles)
+        sin2 = jnp.sin(angles) * jnp.where(jnp.arange(head_dim) < half, -1.0, 1.0)
         pos = seq_lens - lax.axis_index("sp") * seq_blk
-        reps = 16 // kv_loc
         flat = (batch_rows, seq_blk * kv_loc, head_dim)
-        k_out, v_out, o, ml = attention(
-            pos, q_rot, jnp.tile(k_rot, (1, reps, 1)), jnp.tile(v_new, (1, reps, 1)), k_blk.reshape(flat), v_blk.reshape(flat)
+        k_out, v_out, o, ml = front(
+            pos, x_tok, g_attn.reshape(1, -1), cos2, sin2, wq_loc, wk_loc, wv_loc, k_blk.reshape(flat), v_blk.reshape(flat)
         )
         y_out = tail(o, ml, x_tok, g_mlp.reshape(1, -1), wo_loc, wg_loc, wu_loc, wd_loc)
         return y_out, k_out.reshape(k_blk.shape), v_out.reshape(v_blk.shape)

time: 154 us -> 135 us (0.88)
  matrix products: 13.6 us -> 0 us
  other arithmetic: 7.16 us -> 2.67 us
  local copies, waits for them, and re-layouts: 8.04 us -> 5.73 us
  Pallas kernels: 124 us -> 126 us
    dot_general x3 -> x0, matrix products: 13.6 us -> none  [the longest x1 8.78 us: local_step(): jnp.dot(x_norm, wq_loc, preferred_element_type=F32).astype(BF16)]
    another operation x3 -> x0, local copies, waits for them, and re-layouts: 2.63 us -> none  [the longest x2 1.33 us: local_step(): jnp.tile(v_new, (1, reps, 1))]
    pallas_call x1, Pallas kernels: 33.8 us -> 35.9 us  [front(): pl.pallas_call(front_kernel, name='front', in_specs=[pl.BlockSpec(memory_...]
    reduce_sum x1 -> x0, other arithmetic: 2.08 us -> none  [rms_norm(): jnp.mean(x_f32 * x_f32, axis=-1, keepdims=True) + NORM_EPS]
    concatenate x2 -> x0, other arithmetic: 1.9 us -> none  [apply_rope(): jnp.concatenate([first_half * cos_a - second_half * sin_a, second_half *...]
    unnamed x12 -> x1, local copies, waits for them, and re-layouts: 4.62 us -> 3.13 us
where the time goes in v2:
time: 135 us
  Pallas kernels  126 us (93%)
  local copies, waits for them, and re-layouts  5.73 us (4%)
  other arithmetic  2.67 us (2%)
    pallas_call x1, Pallas kernels, tail(): pl.pallas_call(tail_kernel, name='tail', out_shape=jax.ShapeDtypeStruct((...  90.2 us
    pallas_call x1, Pallas kernels, front(): pl.pallas_call(front_kernel, name='front', in_specs=[pl.BlockSpec(memory_...  35.9 us
    unnamed x1, local copies, waits for them, and re-layouts  3.13 us

profile of v2, /device:TPU:0, one launch (start us, length us, event | category | flops | bytes accessed | tf_op | source)
XLA Modules:
  0.0 135.2 jit_solution(12108996668776437669)
XLA Ops:
  0.6 0.1 compare_select_fusion
  0.7 1.4 fusion.1
  2.1 1.3 reshape.31.g_ref
  3.4 1.3 reshape.34.g_ref
  4.7 1.2 fusion
  5.9 35.9 %front.1 = (bf16[256,256,128]{2,1,0:T(8,128)(2,1)}, bf16[256,256,128]{2,1,0:T(8,128)(2,1)}, f32[4,2,64,8,128]{4,3,2,1,0:T(8,128)}, f32[4,2,2,8,128]{4,3,2,1,0:T(8,128)}) custom-call(s32[256]{0:T(256)} %get-tuple-element.14.pos_ref, bf16[256,4096]{1,0:T(8,128)(2,1)} %x_ref.3, bf16[1,4096]{1,0:T(2,128)(2,1)} %reshape.31.g_ref, ...), custom_call_target="tpu_custom_call" | custom-call | flops 10000000000 | bytes 100000000 | tf_op jit(solution)/shard_map/front/pallas_call | solution.py:173
  41.9 90.2 %tail.1 = bf16[256,4096]{1,0:T(8,128)(2,1)} custom-call(f32[4,2,64,8,128]{4,3,2,1,0:T(8,128)} %get-tuple-element.7.o_ref, f32[4,2,2,8,128]{4,3,2,1,0:T(8,128)} %get-tuple-element.8.ml_ref, bf16[256,4096]{1,0:T(8,128)(2,1)} %x_ref.3, bf16[1,4096]{1,0:T(2,128)(2,1)} %reshape.34.g_ref, bf16[2048,4096]{1,0:T(8,128)(2,1)} %wo_hbm.1, bf16[4096,7168]{1,0:T(8,128)(2,1)} %wg_hbm.1, ...), custom_call_target="tpu_custom_call" | custom-call | flops 10000000000 | bytes 100000000 | tf_op jit(solution)/shard_map/tail/pallas_call | solution.py:432
  132.1 3.1 %copy.17 = bf16[256,4096]{1,0:T(8,128)(2,1)} copy(bf16[256,4096]{1,0:T(8,128)(2,1)} %tail.1) | data formatting | bytes 4194304
  (1 shorter events, 0.0 us)

commit v3 on v2

v3 whole, which is shorter than its diff:
```python
import functools

import jax
import jax.numpy as jnp
from jax import lax
from jax.experimental import pallas as pl
from jax.experimental.pallas import tpu as pltpu
from jax.sharding import PartitionSpec as P

ROPE_BASE = 500000.0
NORM_EPS = 1e-5
F32 = jnp.float32
BF16 = jnp.bfloat16
MESH = pl.DeviceIdType.MESH
VMEM_LIMIT = 67_000_000

ROWS_STEP = 16
CHUNK = 512
RING = 6
SLOTS = 20
ORDERS = ("zxy", "yzx", "zxy", "xyz", "zxy", "yzx", "zxy", "yzx")


def front_kernel(pos_ref, x_ref, g_ref, cos_ref, sin_ref, wq_hbm, wk_hbm, wv_hbm, k_hbm, v_hbm,
                 ko_hbm, vo_hbm, o_ref, ml_ref, xn, w_v, qf, kf, vf, kbuf, vbuf, w_sem, in_sem, out_sem):
    batch = x_ref.shape[0]
    rows, dim = k_hbm.shape[1:]
    kv = rows // 64
    heads = wq_hbm.shape[1] // dim
    group = heads // kv
    scale = dim**-0.5
    steps = batch // ROWS_STEP
    q_tiles, k_tiles = wq_hbm.shape[1] // 256, wk_hbm.shape[1] // 256

    weights = [(wq_hbm, j) for j in range(q_tiles)] + [(wk_hbm, j) for j in range(k_tiles)] + [(wv_hbm, j) for j in range(k_tiles)]
    for t, (ref, j) in enumerate(weights):
        pltpu.make_async_copy(ref.at[:, pl.ds(j * 256, 256)], w_v.at[t], w_sem.at[t]).start()

    def block_in(t, slot):
        at = pl.ds(pl.multiple_of(t * ROWS_STEP, ROWS_STEP), ROWS_STEP)
        return (
            pltpu.make_async_copy(k_hbm.at[at], kbuf.at[slot], in_sem.at[0, slot]),
            pltpu.make_async_copy(v_hbm.at[at], vbuf.at[slot], in_sem.at[1, slot]),
        )

    def block_out(t, slot):
        at = pl.ds(pl.multiple_of(t * ROWS_STEP, ROWS_STEP), ROWS_STEP)
        return (
            pltpu.make_async_copy(kbuf.at[slot], ko_hbm.at[at], out_sem.at[0, slot]),
            pltpu.make_async_copy(vbuf.at[slot], vo_hbm.at[at], out_sem.at[1, slot]),
        )

    for t in range(RING):
        for copy in block_in(t, t):
            copy.start()

    def norm_step(j, carry):
        at = pl.ds(pl.multiple_of(j * 32, 32), 32)
        x = x_ref[at, :].astype(F32)
        r = lax.rsqrt(jnp.mean(x * x, axis=-1, keepdims=True) + NORM_EPS)
        xn[at, :] = (x * r * g_ref[0:1, :]).astype(BF16)
        return carry

    lax.fori_loop(0, batch // 32, norm_step, 0)

    def project(t):
        pltpu.make_async_copy(wk_hbm.at[:, pl.ds(0, 256)], w_v.at[t], w_sem.at[t]).wait()
        return jnp.dot(xn[...], w_v[t], preferred_element_type=F32).astype(BF16).astype(F32)

    def rotate(head):
        return (head * cos_ref[...] + pltpu.roll(head, dim // 2, 1) * sin_ref[...]).astype(BF16).astype(F32)

    def q_step(t, carry):
        y = project(t)
        for j in range(2):
            qf[pl.ds(2 * t + j, batch, stride=heads), :] = rotate(y[:, j * dim : (j + 1) * dim])
        return carry

    def k_step(t, carry):
        y = project(q_tiles + t)
        for j in range(2):
            head = rotate(y[:, j * dim : (j + 1) * dim])
            for rep in range(16 // kv):
                kf[pl.ds(rep * kv + 2 * t + j, batch, stride=16), :] = head
        return carry

    def v_step(t, carry):
        y = project(q_tiles + k_tiles + t)
        for j in range(2):
            for rep in range(16 // kv):
                vf[pl.ds(rep * kv + 2 * t + j, batch, stride=16), :] = y[:, j * dim : (j + 1) * dim]
        return carry

    lax.fori_loop(0, q_tiles, q_step, 0)
    lax.fori_loop(0, k_tiles, k_step, 0)
    lax.fori_loop(0, k_tiles, v_step, 0)

    ml_ref[...] = jnp.zeros_like(ml_ref)
    row16 = lax.broadcasted_iota(jnp.int32, (16, dim), 0)
    row_id = lax.broadcasted_iota(jnp.int32, (heads, rows), 0)
    col_id = lax.broadcasted_iota(jnp.int32, (heads, rows), 1)
    same_head = (col_id % kv) == (row_id // group)
    col_id = jnp.where(same_head, col_id, rows * 1024)
    lane = lax.broadcasted_iota(jnp.int32, (heads, 128), 1)
    per = 64 // ROWS_STEP

    def attend_step(t, carry):
        slot = lax.rem(t, RING)
        chip, part = lax.div(t, per), lax.rem(t, per)
        for copy in block_in(t, slot):
            copy.wait()
        for b in range(ROWS_STEP):
            first = pos_ref[t * ROWS_STEP + b] * kv
            start = pl.multiple_of(jnp.clip(first // 16, 0, rows // 16 - 1) * 16, 16)
            lo = first - start
            here = (row16 >= lo) & (row16 < lo + kv)
            new = pl.ds(pl.multiple_of((t * ROWS_STEP + b) * 16, 16), 16)
            at = pl.ds(start, 16)
            kbuf[slot, b, at, :] = jnp.where(here, kf[new, :].astype(BF16), kbuf[slot, b, at, :])
            vbuf[slot, b, at, :] = jnp.where(here, vf[new, :].astype(BF16), vbuf[slot, b, at, :])
        maxes = jnp.concatenate([ml_ref[chip, 0, 0], ml_ref[chip, 1, 0]], axis=0)
        sums = jnp.concatenate([ml_ref[chip, 0, 1], ml_ref[chip, 1, 1]], axis=0)
        for base in range(0, ROWS_STEP, 8):
            scores, weights = [], []
            for b in range(base, base + 8):
                q = qf[pl.ds(pl.multiple_of((t * ROWS_STEP + b) * heads, heads), heads), :].astype(BF16)
                s = lax.dot_general(q, kbuf[slot, b], (((1,), (1,)), ((), ())), preferred_element_type=F32)
                scores.append(s * scale)
            for n, b in enumerate(range(base, base + 8)):
                valid = col_id < (pos_ref[t * ROWS_STEP + b] + 1) * kv
                s = jnp.where(valid, scores[n], -1e30)
                m = jnp.max(s, axis=1, keepdims=True)
                w = jnp.where(valid, jnp.exp(s - m), 0.0)
                here = lane == part * ROWS_STEP + b
                maxes = jnp.where(here, m, maxes)
                sums = jnp.where(here, jnp.sum(w, axis=1, keepdims=True), sums)
                weights.append(w.astype(BF16))
            for n, b in enumerate(range(base, base + 8)):
                o = jnp.dot(weights[n], vbuf[slot, b], preferred_element_type=F32)
                o_ref[chip, 0, part * ROWS_STEP + b] = o[:8]
                o_ref[chip, 1, part * ROWS_STEP + b] = o[8:]
        ml_ref[chip, 0, 0] = maxes[:8]
        ml_ref[chip, 1, 0] = maxes[8:]
        ml_ref[chip, 0, 1] = sums[:8]
        ml_ref[chip, 1, 1] = sums[8:]
        for copy in block_out(t, slot):
            copy.start()

        @pl.when((t >= 1) & (t - 1 + RING < steps))
        def _():
            before = lax.rem(t - 1, RING)
            for copy in block_out(t - 1, before):
                copy.wait()
            for copy in block_in(t - 1 + RING, before):
                copy.start()

        return carry

    lax.fori_loop(0, steps, attend_step, 0)
    for t in range(steps - RING, steps):
        for copy in block_out(t, t % RING):
            copy.wait()


def front(pos, x_tok, g_attn, cos2, sin2, wq, wk, wv, k_blk, v_blk):
    batch, width = x_tok.shape
    _, rows, dim = k_blk.shape
    heads = wq.shape[1] // dim
    tiles = (wq.shape[1] + wk.shape[1] + wv.shape[1]) // 256
    vmem = pl.BlockSpec(memory_space=pltpu.VMEM)
    hbm = pl.BlockSpec(memory_space=pl.ANY)
    dma = pltpu.SemaphoreType.DMA
    return pl.pallas_call(
        front_kernel,
        name="front",
        in_specs=[pl.BlockSpec(memory_space=pltpu.SMEM), vmem, vmem, vmem, vmem, hbm, hbm, hbm, hbm, hbm],
        out_specs=[hbm, hbm, vmem, vmem],
        out_shape=[
            jax.ShapeDtypeStruct(k_blk.shape, BF16),
            jax.ShapeDtypeStruct(v_blk.shape, BF16),
            jax.ShapeDtypeStruct((batch // 64, 2, 64, 8, dim), F32),
            jax.ShapeDtypeStruct((batch // 64, 2, 2, 8, dim), F32),
        ],
        scratch_shapes=[
            pltpu.VMEM((batch, width), BF16),
            pltpu.VMEM((tiles, width, 256), BF16),
            pltpu.VMEM((batch * heads, dim), F32), pltpu.VMEM((batch * 16, dim), F32), pltpu.VMEM((batch * 16, dim), F32),
            pltpu.VMEM((RING, ROWS_STEP, rows, dim), BF16), pltpu.VMEM((RING, ROWS_STEP, rows, dim), BF16),
            dma((tiles,)), dma((2, RING)), dma((2, RING)),
        ],
        compiler_params=pltpu.CompilerParams(vmem_limit_bytes=VMEM_LIMIT),
        cost_estimate=pl.CostEstimate(flops=10**10, bytes_accessed=10**8, transcendentals=0),
    )(pos, x_tok, g_attn, cos2, sin2, wq, wk, wv, k_blk, v_blk)


def blend(first, count, pairs, out_ref):
    for b in range(count):
        total = None
        for weight, part in pairs:
            term = jnp.broadcast_to(weight[:, first + b : first + b + 1], (8, 128)) * part[b]
            total = term if total is None else total + term
        out_ref[b] = total


def tail_kernel(o_ref, ml_ref, g_ref, x_hbm, wo_hbm, wg_hbm, wu_hbm, wd_hbm, y_ref,
                r1, rm1, snd, sndm, r2, rm2, attn, attn_bf, part_o, got_o, sum_o, got_z, x_rows, hid, zb,
                ring, act, acc, got_a, sum_a, got_b, yall,
                x_sem, wo_sem, w_sem, s1, t1, s1m, t1m, s2, t2, s2m, t2m, so, to, sz, tz, sh, th, sa, ta, sb, tb, sg, tg, sd, td):
    sp = lax.axis_index("sp")
    z = lax.axis_index("tp")
    c = sp % 2
    xx = (sp // 2) % 2
    yy = sp // 4
    chip = sp // 2
    depth = attn_bf.shape[1]
    model = acc.shape[1]
    width = act.shape[1]
    tiles, pieces = width // 256, model // 256
    first_item = pieces * depth // ring.shape[1]

    def wo_copy(j):
        src = wo_hbm.at[pl.ds(pl.multiple_of(c * depth, depth), depth), pl.ds(j * 256, 256)]
        per = ring.shape[1] // depth
        return pltpu.make_async_copy(src, ring.at[j // per, pl.ds((j % per) * depth, depth)], wo_sem.at[j])

    def up_copy(hbm, t, slot):
        at = pl.ds(pl.multiple_of(c * width + t * 256, 256), 256)
        return pltpu.make_async_copy(hbm.at[:, at], ring.at[slot], w_sem.at[slot])

    def down_copy(j, slot):
        src = wd_hbm.at[pl.ds(pl.multiple_of(c * width, width), width), pl.ds(pl.multiple_of(j * 256, 256), 256)]
        return pltpu.make_async_copy(src, ring.at[slot, pl.ds(0, width)], w_sem.at[slot])

    for j in range(pieces):
        wo_copy(j).start()
    for n in range(first_item, SLOTS):
        up_copy(wu_hbm if (n - first_item) % 2 else wg_hbm, (n - first_item) // 2, n).start()
    x_copies = []
    for half in range(2):
        at = pl.ds(pl.multiple_of(chip * 64 + half * 32 + c * 16, 16), 16)
        x_copies.append(pltpu.make_async_copy(x_hbm.at[at, :], x_rows.at[half], x_sem.at[half]))
        x_copies[half].start()

    def spi(fx, fy, fc):
        px = 1 - xx if fx else xx
        py = 1 - yy if fy else yy
        pc = 1 - c if fc else c
        return (py * 2 + px) * 2 + pc

    core_id = {"sp": spi(0, 0, 1)}
    x_id = {"sp": spi(1, 0, 0)}
    y_id = {"sp": spi(0, 1, 0)}
    d_id = {"sp": spi(1, 1, 0)}
    z_id = {"tp": 1 - z}

    barrier = pltpu.get_barrier_semaphore()
    for peer in (core_id, x_id, y_id, d_id, z_id):
        pl.semaphore_signal(barrier, inc=1, device_id=peer, device_id_type=MESH)
    pl.semaphore_wait(barrier, 5)

    sent = []

    def send(src, dst, send_sem, recv_sem, peer):
        copy = pltpu.make_async_remote_copy(src_ref=src, dst_ref=dst, send_sem=send_sem, recv_sem=recv_sem, device_id=peer, device_id_type=MESH)
        copy.start()
        sent.append(copy)
        return copy

    groups = [(1 - yy) * 2 + (1 - xx), yy * 2 + (1 - xx), (1 - yy) * 2 + xx, chip]
    peers = [d_id, x_id, y_id]
    first, stats = {}, []
    for half in range(2):
        rows = pl.ds(half * 32, 32)
        for k in range(4):
            if half == 0:
                stats.append(send(ml_ref.at[groups[k], 1 - c], rm1.at[k], s1m.at[k], t1m.at[k], core_id))
            first[half, k] = send(o_ref.at[groups[k], 1 - c, rows], r1.at[k, rows], s1.at[half, k], t1.at[half, k], core_id)
    second, stats2, factors = {}, [], []
    for half in range(2):
        rows = pl.ds(half * 32, 32)
        for k in range(4):
            if half == 0:
                stats[k].wait_recv()
                m0, m1 = ml_ref[groups[k], c, 0], rm1[k, 0]
                m = jnp.maximum(m0, m1)
                f0, f1 = jnp.exp(m0 - m), jnp.exp(m1 - m)
                factors.append((f0, f1))
                sndm[k, 0] = m
                sndm[k, 1] = f0 * ml_ref[groups[k], c, 1] + f1 * rm1[k, 1]
                if k < 3:
                    stats2.append(send(sndm.at[k], rm2.at[k], s2m.at[k], t2m.at[k], peers[k]))
            first[half, k].wait_recv()
            f0, f1 = factors[k]
            blend(half * 32, 32, [(f0, o_ref.at[groups[k], c, rows]), (f1, r1.at[k, rows])], snd.at[k, rows])
            if k < 3:
                second[half, k] = send(snd.at[k, rows], r2.at[k, rows], s2.at[half, k], t2.at[half, k], peers[k])

    to_z, shares = [], None
    for half in range(2):
        rows = pl.ds(half * 32, 32)
        if half == 0:
            for k in range(3):
                stats2[k].wait_recv()
            ms = [sndm[3, 0]] + [rm2[k, 0] for k in range(3)]
            m = functools.reduce(jnp.maximum, ms)
            fs = [jnp.exp(v - m) for v in ms]
            total = fs[0] * sndm[3, 1] + fs[1] * rm2[0, 1] + fs[2] * rm2[1, 1] + fs[3] * rm2[2, 1]
            total = jnp.where(total > 0.0, total, 1.0)
            shares = [f / total for f in fs]
        for k in (1, 2, 0):
            second[half, k].wait_recv()
        blend(half * 32, 32, [(shares[0], snd.at[3, rows])] + [(shares[k + 1], r2.at[k, rows]) for k in range(3)], attn)
        for h in range(8):
            attn_bf[:, h * 128 : (h + 1) * 128] = attn[:, h, :].astype(BF16)
        if half == 0:
            for j in range(pieces):
                wo_copy(j).wait()
        per = ring.shape[1] // depth

        def wo_step(n, carry):
            for k in range(per):
                at = pl.ds(pl.multiple_of((n * per + k) * 256, 256), 256)
                part_o[half, :, at] = jnp.dot(attn_bf[...], ring[n, k * depth : (k + 1) * depth, :], preferred_element_type=F32)
            return carry

        lax.fori_loop(0, first_item, wo_step, 0)
        mine = pl.ds(pl.multiple_of(c * 16, 16), 16)
        other = pl.ds(pl.multiple_of((1 - c) * 16, 16), 16)
        copy = send(part_o.at[half, other], got_o.at[half], so.at[half], to.at[half], core_id)
        if half == 1:
            for n in range(SLOTS, SLOTS + first_item):
                up_copy(wu_hbm if (n - first_item) % 2 else wg_hbm, (n - first_item) // 2, n - SLOTS).start()
        copy.wait_recv()
        sum_o[half] = part_o[half, mine] + got_o[half]
        to_z.append(send(sum_o.at[half], got_z.at[half], sz.at[half], tz.at[half], z_id))
    to_core = []
    for half in range(2):
        to_z[half].wait_recv()
        x_copies[half].wait()
        hid[half, c] = (x_rows[half].astype(F32) + (sum_o[half] + got_z[half])).astype(BF16).astype(F32)
        to_core.append(send(hid.at[half, c], hid.at[half, c], sh.at[half], th.at[half], core_id))
    for half in range(2):
        to_core[half].wait_recv()

    for cc in range(2):
        for zz in range(2):
            h = jnp.concatenate([hid[0, cc, zz * 8 : zz * 8 + 8, :], hid[1, cc, zz * 8 : zz * 8 + 8, :]], axis=0)
            r = lax.rsqrt(jnp.mean(h * h, axis=-1, keepdims=True) + NORM_EPS)
            zb[(cc * 2 + zz) * 16 : (cc * 2 + zz) * 16 + 16, :] = (h * r * g_ref[1:2, :]).astype(BF16)

    def up_step(t, carry):
        n = first_item + 2 * t
        slots = [lax.rem(n, SLOTS), lax.rem(n + 1, SLOTS)]
        up_copy(wg_hbm, t, slots[0]).wait()
        gate = jnp.dot(zb[...], ring[slots[0]], preferred_element_type=F32).astype(BF16).astype(F32)
        up_copy(wu_hbm, t, slots[1]).wait()
        up = jnp.dot(zb[...], ring[slots[1]], preferred_element_type=F32).astype(BF16).astype(F32)
        act[:, pl.ds(pl.multiple_of(t * 256, 256), 256)] = (gate * jax.nn.sigmoid(gate) * up).astype(BF16)
        later = n + SLOTS - first_item

        @pl.when(later < 2 * tiles)
        def _():
            up_copy(wg_hbm, later // 2, slots[0]).start()
            up_copy(wu_hbm, later // 2, slots[1]).start()

        @pl.when((later >= 2 * tiles) & (later < 2 * tiles + pieces))
        def _():
            down_copy(later - 2 * tiles, slots[0]).start()
            down_copy(later + 1 - 2 * tiles, slots[1]).start()

        return carry

    lax.fori_loop(0, tiles, up_step, 0)

    mine = pl.ds(pl.multiple_of(c * 32, 32), 32)
    other = pl.ds(pl.multiple_of((1 - c) * 32, 32), 32)
    zmine = pl.ds(pl.multiple_of(z * 16, 16), 16)
    zother = pl.ds(pl.multiple_of((1 - z) * 16, 16), 16)
    ids = {"x": x_id, "y": y_id, "z": z_id}

    def rows_of(flips):
        px = 1 - xx if "x" in flips else xx
        py = 1 - yy if "y" in flips else yy
        pz = 1 - z if "z" in flips else z
        block = ((py * 2 + px) * 2 + c) * 2 + pz
        return pl.ds(pl.multiple_of(block * 16, 16), 16)

    def columns(n):
        return pl.ds(n * CHUNK, CHUNK)

    def gather_send(n, idx):
        d0, d1, d2 = ORDERS[n]
        src = ["", "", d0, "", d0, d1, d0 + d1][idx]
        along = [d0, d1, d1, d2, d2, d2, d2][idx]
        ref = yall.at[rows_of(src), columns(n)]
        gathers.append(pltpu.make_async_remote_copy(src_ref=ref, dst_ref=ref, send_sem=sg.at[n, idx], recv_sem=tg.at[n, idx], device_id=ids[along], device_id_type=MESH))
        gathers[-1].start()

    def landed(n, idx):
        d0, d1, d2 = ORDERS[n]
        return [d0, d1, d0 + d1, d2, d2 + d0, d2 + d1, d0 + d1 + d2][idx]

    def core_send(n, j):
        ref = yall.at[rows_of("" if j == 0 else landed(n, j - 1)), columns(n)]
        gathers.append(pltpu.make_async_remote_copy(src_ref=ref, dst_ref=ref, send_sem=sd.at[n, j], recv_sem=td.at[n, j], device_id=core_id, device_id_type=MESH))
        gathers[-1].start()

    def gather_wait(n, idx):
        ref = yall.at[rows_of(landed(n, idx)), columns(n)]
        pltpu.make_async_remote_copy(src_ref=ref, dst_ref=ref, send_sem=sg.at[n, idx], recv_sem=tg.at[n, idx], device_id=core_id, device_id_type=MESH).wait_recv()

    def core_wait(n, j):
        ref = yall.at[rows_of(""), columns(n)]
        pltpu.make_async_remote_copy(src_ref=ref, dst_ref=ref, send_sem=sd.at[n, j], recv_sem=td.at[n, j], device_id=core_id, device_id_type=MESH).wait_recv()

    gathers, to_a, to_b = [], {}, {}
    chunks = model // CHUNK
    per = CHUNK // 256

    def stage0(n):
        for k in range(per):
            j = n * per + k
            item = first_item + 2 * tiles + j
            slot = item % SLOTS
            down_copy(j, slot).wait()
            acc[:, j * 256 : (j + 1) * 256] = jnp.dot(act[...], ring[slot, 0:width, :], preferred_element_type=F32)
            later = item + SLOTS - first_item - 2 * tiles
            if later < pieces:
                down_copy(later, slot).start()
        to_a[n] = send(acc.at[other, columns(n)], got_a.at[:, columns(n)], sa.at[n], ta.at[n], core_id)

    def stage1(n):
        to_a[n].wait_recv()
        sum_a[:, columns(n)] = acc[mine, columns(n)] + got_a[:, columns(n)]
        to_b[n] = send(sum_a.at[zother, columns(n)], got_b.at[:, columns(n)], sb.at[n], tb.at[n], z_id)

    def stage2(n):
        to_b[n].wait_recv()
        own = pl.ds(pl.multiple_of(z * 8, 8), 8)
        h = jnp.concatenate([hid[0, c, own, columns(n)], hid[1, c, own, columns(n)]], axis=0)
        yall[rows_of(""), columns(n)] = (h + (sum_a[zmine, columns(n)] + got_b[:, columns(n)])).astype(BF16).astype(F32)
        for idx in (0, 1, 3):
            gather_send(n, idx)
        core_send(n, 0)

    def stage3(n):
        gather_wait(n, 0)
        gather_send(n, 2)
        gather_send(n, 4)
        core_send(n, 1)
        gather_wait(n, 1)
        gather_send(n, 5)
        core_send(n, 2)

    def stage4(n):
        gather_wait(n, 2)
        gather_send(n, 6)
        core_send(n, 3)

    def stage5(n):
        for idx in (3, 4, 5, 6):
            gather_wait(n, idx)
            core_send(n, idx + 1)

    def stage6(n):
        for j in range(8):
            core_wait(n, j)

    for n in range(chunks + 6):
        for stage, lag in ((stage0, 0), (stage1, 1), (stage2, 2), (stage3, 3), (stage4, 4), (stage5, 5), (stage6, 6)):
            if 0 <= n - lag < chunks:
                stage(n - lag)

    def finish(g, carry):
        block = lax.div(g, 4) * 4 + lax.rem(g, 2) * 2
        half = lax.rem(lax.div(g, 2), 2)
        parts = [yall[pl.ds(pl.multiple_of((block + zz) * 16 + half * 8, 8), 8), :] for zz in range(2)]
        y_ref[pl.ds(pl.multiple_of(g * 16, 16), 16), :] = jnp.concatenate(parts, axis=0).astype(BF16)
        return carry

    lax.fori_loop(0, y_ref.shape[0] // 16, finish, 0)
    for copy in sent + gathers:
        copy.wait_send()


def tail(o, ml, gains, x_tok, wo, wg, wu, wd):
    batch, width = x_tok.shape
    depth = wo.shape[0] // 2
    quarter = wg.shape[1] // 2
    vmem = pl.BlockSpec(memory_space=pltpu.VMEM)
    hbm = pl.BlockSpec(memory_space=pl.ANY)
    dma = pltpu.SemaphoreType.DMA
    heads = (64, 8, 128)
    stat = (2, 8, 128)
    chunks = width // CHUNK
    return pl.pallas_call(
        tail_kernel,
        name="tail",
        out_shape=jax.ShapeDtypeStruct((batch, width), BF16),
        in_specs=[vmem, vmem, vmem, hbm, hbm, hbm, hbm, hbm],
        out_specs=vmem,
        scratch_shapes=[
            pltpu.VMEM((4, *heads), F32), pltpu.VMEM((4, *stat), F32),
            pltpu.VMEM((4, *heads), F32), pltpu.VMEM((4, *stat), F32),
            pltpu.VMEM((3, *heads), F32), pltpu.VMEM((3, *stat), F32),
            pltpu.VMEM((32, 8, 128), F32), pltpu.VMEM((32, depth), BF16),
            pltpu.VMEM((2, 32, width), F32), pltpu.VMEM((2, 16, width), F32), pltpu.VMEM((2, 16, width), F32), pltpu.VMEM((2, 16, width), F32),
            pltpu.VMEM((2, 16, width), BF16), pltpu.VMEM((2, 2, 16, width), F32), pltpu.VMEM((64, width), BF16),
            pltpu.VMEM((SLOTS, width, 256), BF16), pltpu.VMEM((64, quarter), BF16),
            pltpu.VMEM((64, width), F32), pltpu.VMEM((32, width), F32), pltpu.VMEM((32, width), F32), pltpu.VMEM((16, width), F32),
            pltpu.VMEM((batch, width), F32),
            dma((2,)), dma((width // 256,)), dma((SLOTS,)),
            dma((2, 4)), dma((2, 4)), dma((4,)), dma((4,)), dma((2, 3)), dma((2, 3)), dma((3,)), dma((3,)),
            dma((2,)), dma((2,)), dma((2,)), dma((2,)), dma((2,)), dma((2,)),
            dma((chunks,)), dma((chunks,)), dma((chunks,)), dma((chunks,)),
            dma((chunks, 7)), dma((chunks, 7)), dma((chunks, 8)), dma((chunks, 8)),
        ],
        compiler_params=pltpu.CompilerParams(collective_id=0, has_side_effects=True, vmem_limit_bytes=VMEM_LIMIT),
        cost_estimate=pl.CostEstimate(flops=10**10, bytes_accessed=10**8, transcendentals=0),
    )(o, ml, gains, x_tok, wo, wg, wu, wd)


def solution(mesh):
    cache_spec = P(None, "sp", "tp", None)
    col_spec = P(None, "tp")
    row_spec = P("tp", None)
    full_spec = P()

    def local_step(x_tok, seq_lens, k_blk, v_blk, g_attn, wq_loc, wk_loc, wv_loc, wo_loc, g_mlp, wg_loc, wu_loc, wd_loc):
        batch_rows, seq_blk, kv_loc, head_dim = k_blk.shape
        gains = jnp.stack([g_attn, g_mlp]).astype(F32)
        half = head_dim // 2
        inv_freq = jnp.power(F32(ROPE_BASE), jnp.arange(half, dtype=F32) * (-2.0 / head_dim))
        angles = seq_lens.astype(F32)[:, None] * jnp.concatenate([inv_freq, inv_freq])
        cos2 = jnp.cos(angles)
        sin2 = jnp.sin(angles) * jnp.where(jnp.arange(head_dim) < half, -1.0, 1.0)
        pos = seq_lens - lax.axis_index("sp") * seq_blk
        flat = (batch_rows, seq_blk * kv_loc, head_dim)
        k_out, v_out, o, ml = front(
            pos, x_tok, gains, cos2, sin2, wq_loc, wk_loc, wv_loc, k_blk.reshape(flat), v_blk.reshape(flat)
        )
        y_out = tail(o, ml, gains, x_tok, wo_loc, wg_loc, wu_loc, wd_loc)
        return y_out, k_out.reshape(k_blk.shape), v_out.reshape(v_blk.shape)

    return jax.shard_map(local_step, mesh=mesh, in_specs=(full_spec, full_spec, cache_spec, cache_spec, full_spec, col_spec, col_spec, col_spec, row_spec, full_spec, col_spec, col_spec, row_spec), out_specs=(full_spec, cache_spec, cache_spec), check_vma=False)
```

time: 135 us -> 138 us (1.022)
  Pallas kernels: 126 us -> 128 us
    reshape x2 -> x0, local copies, waits for them, and re-layouts: 2.61 us -> none  [the longest x1 1.3 us: local_step(): g_attn.reshape(1, -1)]
    pallas_call x1, Pallas kernels: 90.2 us -> 92.5 us  [tail(): pl.pallas_call(tail_kernel, name='tail', out_shape=jax.ShapeDtypeStruct((...]
    another operation x0 -> x2, local copies, waits for them, and re-layouts: none -> 1.42 us  [local_step(): gains = jnp.stack([g_attn, g_mlp]).astype(F32)]
where the time goes in v3:
time: 138 us; the launch traced here: 137 us
  Pallas kernels  128 us (93%)
  local copies, waits for them, and re-layouts  4.55 us (3%)
  other arithmetic  3.31 us (2%)
    pallas_call x1, Pallas kernels, tail(): pl.pallas_call(tail_kernel, name='tail', out_shape=jax.ShapeDtypeStruct((...  92.5 us
    pallas_call x1, Pallas kernels, front(): pl.pallas_call(front_kernel, name='front', in_specs=[pl.BlockSpec(memory_...  36 us
    unnamed x1, local copies, waits for them, and re-layouts  3.13 us

profile of v3, /device:TPU:0, one launch (start us, length us, event | category | flops | bytes accessed | tf_op | source)
XLA Modules:
  0.0 137.0 jit_solution(8155247229206160796)
XLA Ops:
  0.6 0.1 compare_select_fusion
  0.7 1.3 fusion.1
  2.1 0.7 stack.9
  2.8 0.7 stack.10
  3.5 0.6 maximum_convert_fusion.g_ref
  4.1 1.2 fusion
  5.4 36.0 %front.1 = (bf16[256,256,128]{2,1,0:T(8,128)(2,1)}, bf16[256,256,128]{2,1,0:T(8,128)(2,1)}, f32[4,2,64,8,128]{4,3,2,1,0:T(8,128)}, f32[4,2,2,8,128]{4,3,2,1,0:T(8,128)}) custom-call(s32[256]{0:T(256)} %get-tuple-element.14.pos_ref, bf16[256,4096]{1,0:T(8,128)(2,1)} %x_hbm.1, f32[2,4096]{1,0:T(2,128)} %maximum_convert_fusion.g_ref, ...), custom_call_target="tpu_custom_call" | custom-call | flops 10000000000 | bytes 100000000 | tf_op jit(solution)/shard_map/front/pallas_call | solution.py:173
  41.3 92.5 %tail.1 = bf16[256,4096]{1,0:T(8,128)(2,1)} custom-call(f32[4,2,64,8,128]{4,3,2,1,0:T(8,128)} %get-tuple-element.7.o_ref, f32[4,2,2,8,128]{4,3,2,1,0:T(8,128)} %get-tuple-element.8.ml_ref, f32[2,4096]{1,0:T(2,128)} %maximum_convert_fusion.g_ref, bf16[256,4096]{1,0:T(8,128)(2,1)} %x_hbm.1, bf16[2048,4096]{1,0:T(8,128)(2,1)} %wo_hbm.1, ...), custom_call_target="tpu_custom_call" | custom-call | flops 10000000000 | bytes 100000000 | tf_op jit(solution)/shard_map/tail/pallas_call | solution.py:496
  133.9 3.1 %copy.17 = bf16[256,4096]{1,0:T(8,128)(2,1)} copy(bf16[256,4096]{1,0:T(8,128)(2,1)} %tail.1) | data formatting | bytes 4194304
  (1 shorter events, 0.0 us)
